TPU v7x, 32 devices: a whole 2x2x4 slice. The times are simulated.
32 devices in a mesh: movie: 16 (over z, y, x), user: 2 (over core).
Axes of the slice: x: 2, y: 2, z: 4, core: 2. Of those that a mesh axis runs over, the one named last changes fastest.
Arguments:
- movie_ids: int32 [128, 128], P(('movie', 'user')), may hold values from 0 to 17919, as said below
- ratings: int32 [128, 128], P(('movie', 'user')), may hold values from 0 to 4
- valid: int32 [128, 128], P(('movie', 'user')), may hold values from 0 to 1, as said below
- weights: bfloat16 [5, 17920, 1024], P(None, 'movie'), may hold values from -0.5 to 0.5
- vis_bias: float32 [5, 17920], P(None, 'movie'), may hold values from -5 to 260
- hid_bias: float32 [1024], replicated, may hold values from -5 to 5
Outputs:
- weight_grad: float32 [5, 17920, 1024], P(None, 'movie')
- visible_grad: float32 [5, 17920], P(None, 'movie')
- hidden_grad: float32 [1024], replicated
- positive_hidden: float32 [128, 1024], P(('movie', 'user'))
Inputs may be any that keep to these rules, and one draw needn't show every extreme that they name: `movie_ids`: movie ids within one user's block are distinct. Of the slots with valid 1 among the users of one device (4 consecutive users), at most 96 name movies of any one block of 1120 consecutive movie ids; in every draw some such block takes exactly 96 from the users of every device. Slots with valid 0 are padding and count nowhere.
All inputs are finite; a program needn't handle non-finite values.
Results may differ from a plain program's by a relative error of at most 0.0054.
Values may be sent and summed in bfloat16 or wider, within the bound.
No kernel may reach another device: no remote copies, remote signals or barrier semaphores. Data moves between devices by JAX's collectives and lax.ppermute only.
A program may use at most 128 MiB of HBM per device.

v0:
```python
import jax
import jax.numpy as jnp
from jax import lax
from jax.sharding import PartitionSpec as P


def reconstruct(hidden_rows, weight_table, bias_row, rated_mask, levels):
    group_rows = hidden_rows.shape[0]
    rating_logits = (
        lax.dot_general(
            hidden_rows, weight_table, (((1,), (1,)), ((), ())), preferred_element_type=jnp.float32
        )
        + bias_row[None, :]
    )
    shaped = rating_logits.reshape(group_rows, levels, -1)
    largest = jnp.max(shaped, axis=1, keepdims=True)
    exponent = jnp.exp(shaped - largest)
    softened = (exponent / jnp.sum(exponent, axis=1, keepdims=True)).astype(jnp.bfloat16)
    return (softened * rated_mask[:, None, :]).reshape(group_rows, -1)


def hidden_phase(visible, weight_table, hid_bias, local_users, device_index):
    combined = jnp.dot(visible, weight_table, preferred_element_type=jnp.float32)
    all_probs = jax.nn.sigmoid(hid_bias[None, :] + lax.psum(combined, "movie"))
    own_rows = lax.dynamic_slice_in_dim(all_probs, device_index * local_users, local_users, 0)
    return (own_rows, all_probs.astype(jnp.bfloat16))


def on_device(movie_ids, ratings, valid, weights, vis_bias, hid_bias):
    owners = lax.axis_size("movie")
    device_index = lax.axis_index("movie")
    local_users, slot_count = movie_ids.shape
    levels, local_movies, hidden = weights.shape
    columns = levels * local_movies
    group_rows = owners * local_users
    capacity = max(2, 3 * local_users * slot_count // owners)
    flat_ids = movie_ids.reshape(-1)
    owner_ids = flat_ids // local_movies
    column_ids = ratings.reshape(-1) * local_movies + flat_ids % local_movies
    user_ids = jnp.arange(local_users * slot_count, dtype=jnp.int32) // slot_count
    usable = valid.reshape(-1) == 1
    matches = (owner_ids[:, None] == jnp.arange(owners, dtype=jnp.int32)[None, :]) & usable[:, None]
    ranking = jnp.cumsum(matches.astype(jnp.int32), axis=0) - 1
    placed = jnp.sum(jnp.where(matches, ranking, 0), axis=1)
    target = jnp.where(usable, owner_ids, owners)
    user_slots = (
        jnp.zeros((owners, capacity), jnp.int32).at[target, placed].set(user_ids, mode="drop")
    )
    column_slots = (
        jnp.full((owners, capacity), -1, jnp.int32).at[target, placed].set(column_ids, mode="drop")
    )
    got_users, got_columns = (
        lax.all_to_all(user_slots, "movie", split_axis=0, concat_axis=0, tiled=True),
        lax.all_to_all(column_slots, "movie", split_axis=0, concat_axis=0, tiled=True),
    )
    user_hot = (got_users[:, :, None] == jnp.arange(local_users, dtype=jnp.int32)).astype(
        jnp.bfloat16
    )
    column_hot = (got_columns[:, :, None] == jnp.arange(columns, dtype=jnp.int32)).astype(
        jnp.bfloat16
    )
    shown = jnp.einsum("ncu,ncj->nuj", user_hot, column_hot, preferred_element_type=jnp.float32)
    shown = shown.reshape(group_rows, columns).astype(jnp.bfloat16)
    rated_mask = jnp.sum(shown.reshape(group_rows, levels, local_movies), axis=1)
    weight_table = weights.reshape(columns, hidden)
    positive_own, positive_group = hidden_phase(
        shown, weight_table, hid_bias, local_users, device_index
    )
    reconstructed_ratings = reconstruct(
        positive_group, weight_table, vis_bias.reshape(columns), rated_mask, levels
    )
    negative_own, negative_group = hidden_phase(
        reconstructed_ratings, weight_table, hid_bias, local_users, device_index
    )
    contract = (((0,), (0,)), ((), ()))
    weight_grad = lax.dot_general(
        shown, positive_group, contract, preferred_element_type=jnp.float32
    )
    weight_grad = weight_grad - lax.dot_general(
        reconstructed_ratings, negative_group, contract, preferred_element_type=jnp.float32
    )
    visible_grad = jnp.sum(shown.astype(jnp.float32), axis=0) - jnp.sum(
        reconstructed_ratings.astype(jnp.float32), axis=0
    )
    weight_grad, visible_grad = lax.psum((weight_grad, visible_grad), "user")
    hidden_grad = lax.psum(jnp.sum(positive_own - negative_own, axis=0), ("movie", "user"))
    return (
        weight_grad.reshape(levels, local_movies, hidden),
        visible_grad.reshape(levels, local_movies),
        hidden_grad,
        positive_own,
    )


def solution(mesh):
    in_specs = (
        P(("movie", "user"), None),
        P(("movie", "user"), None),
        P(("movie", "user"), None),
        P(None, "movie", None),
        P(None, "movie"),
        P(),
    )
    out_specs = (P(None, "movie", None), P(None, "movie"), P(), P(("movie", "user"), None))
    return jax.shard_map(
        on_device, mesh=mesh, in_specs=in_specs, out_specs=out_specs, check_vma=False
    )
```

profile of v0, /device:TPU:0, one launch (start us, length us, event | category | flops | bytes accessed | tf_op | source)
XLA Modules:
  0.0 500.1 jit_solution(16229236096760497218)
XLA Ops:
  7.2 0.7 fusion.32
  7.9 0.7 fusion.31
  8.5 0.7 broadcast_compare_fusion
  9.2 0.7 add_select_fusion.2
  9.9 0.7 fusion.18
  10.7 1.2 reduce-window.6
  11.8 0.2 slice_reduce_fusion
  12.1 0.1 fusion.12
  12.2 0.6 broadcast_in_dim.15
  12.8 71.8 %scatter_fusion.1 = s32[16,96]{1,0:T(8,128)} fusion(s32[16,96]{1,0:T(8,128)} %broadcast_in_dim.15, s32[512]{0:T(512)S(1)} %bitcast.81, s32[512]{0:T(512)S(1)} %get-tuple-element.10), kind=kCustom, calls=%fused_computation.1 | custom fusion | bytes 10240 | tf_op jit(solution)/shard_map/scatter | solution.py:50
  84.6 8.3 %all-to-all-start.1 = ((s32[16,1,96]{2,1,0:T(1,128)}), s32[16,1,96]{2,1,0:T(1,128)S(1)}, u32[]{:S(2)}, u32[]{:S(2)}) async-start(s32[16,1,96]{2,1,0:T(1,128)} %bitcast.13), calls=%async_computation.1 | async-start | bytes 16384 | tf_op jit(solution)/shard_map/all_to_all | solution.py:54
  92.9 0.0 all-reduce.4.cloned.1.call-start
  93.0 25.2 %scatter_fusion = s32[16,96]{1,0:T(8,128)S(1)} fusion(s32[16,96]{1,0:T(8,128)S(1)} %broadcast_in_dim.12, s32[512]{0:T(512)S(1)} %bitcast.82, s32[512]{0:T(512)S(1)} %add_select_fusion.1), kind=kCustom, calls=%fused_computation | custom fusion | bytes 10240 | tf_op jit(solution)/shard_map/scatter | solution.py:47
  118.2 14.0 %all_to_all.18 = s32[16,1,96]{2,1,0:T(1,128)S(1)} all-to-all(s32[16,1,96]{2,1,0:T(1,128)S(1)} %bitcast.75), channel_id=1, replica_groups=mesh['movie'=16,'user'=2] {'movie'}, dimensions={0} | all-to-all | bytes 12288 | tf_op jit(solution)/shard_map/all_to_all | solution.py:53
  132.2 6.6 %convert_reduce_fusion.1 = (f32[5600]{0:T(1024)S(1)}, bf16[16,4,5600]{2,1,0:T(4,128)(2,1)S(1)}) fusion(s32[16,96]{1,0:T(8,128)S(1)} %bitcast.85, s32[16,96]{1,0:T(8,128)S(1)} %bitcast.86), kind=kOutput, calls=%fused_computation.12 | convolution fusion | flops 78490144 | bytes 751488 | tf_op jit(solution)/shard_map/ncu,ncj->nuj/dot_general | solution.py:62
  138.8 0.3 convert_element_type.42
  139.1 7.3 %fusion.24 = f32[64,1024]{1,0:T(8,128)} fusion(bf16[64,5600]{1,0:T(8,128)(2,1)S(1)} %convert_element_type.42, bf16[5600,1024]{1,0:T(8,128)(2,1)} %bitcast.77), kind=kOutput, calls=%fused_computation.65 | convolution fusion | flops 734003200 | bytes 12447744 | tf_op jit(solution)/shard_map/dot_general | solution.py:23
  146.4 0.0 all-reduce.4.cloned.1.call-update
  146.5 0.2 all-reduce.6.cloned.1.call-start
  146.7 0.1 add.98
  146.8 0.9 convert_element_type.45
  147.7 0.8 reduce_sum.62
  148.5 1.1 mul.26
  149.6 2.7 mul.27
  152.4 98.4 %all-reduce.4.cloned.1.call-done = f32[64,1024]{1,0:T(8,128)} async-done(((f32[64,1024]{1,0:T(8,128)}), f32[64,1024]{1,0:T(8,128)}) %all-reduce.4.cloned.1.call-update) | async-done | bytes 262160 | tf_op jit(solution)/shard_map/psum | solution.py:24
  250.7 1.0 add_divide_fusion.1
  251.8 11.1 %fusion.9 = f32[5600,1024]{1,0:T(8,128)} fusion(bf16[64,5600]{1,0:T(8,128)(2,1)} %copy-done.1, f32[64,1024]{1,0:T(8,128)S(1)} %add_divide_fusion.1), kind=kOutput, calls=%fused_computation.22 | convolution fusion | flops 734068736 | bytes 23916544 | tf_op jit(solution)/shard_map/dot_general | solution.py:76
  262.9 4.7 convolution_add_fusion
  267.6 1.9 reshape.182
  269.6 0.7 reduce_max.9
  270.3 1.0 fusion.3
  271.3 0.8 fusion.4
  272.1 7.1 %convolution_bitcast_fusion = f32[64,1024]{1,0:T(8,128)} fusion(bf16[5,1120,1024]{2,1,0:T(8,128)(2,1)} %param.9, bf16[64,5,1120]{2,1,0:T(8,128)(2,1)S(1)} %fusion.4), kind=kOutput, calls=%fused_computation.15 | convolution fusion | flops 734003200 | bytes 12447744 | tf_op jit(solution)/shard_map/dot_general | solution.py:23
  279.2 0.3 all-reduce.8.cloned.1.call-start
  279.4 0.2 sub.51
  279.6 1.6 sub.52
  281.2 1.6 div.54
  282.8 3.0 div.55
  285.8 3.0 convert_reduce_fusion
  288.8 97.3 %all-reduce.6.cloned.1.call-done = f32[64,1024]{1,0:T(8,128)} async-done(((f32[64,1024]{1,0:T(8,128)}), f32[64,1024]{1,0:T(8,128)}) %all-reduce.6.cloned.1.call-update) | async-done | bytes 262160 | tf_op jit(solution)/shard_map/psum | solution.py:24
  386.0 1.0 add_divide_fusion
  387.1 15.5 %convolution_subtract_fusion = f32[5600,1024]{1,0:T(8,128)} fusion(f32[5600,1024]{1,0:T(8,128)} %fusion.9, bf16[64,5600]{1,0:T(8,128)(2,1)} %get-tuple-element.7, f32[64,1024]{1,0:T(8,128)S(1)} %add_divide_fusion), kind=kOutput, calls=%fused_computation.5 | convolution fusion | flops 739803136 | bytes 46854144 | tf_op jit(solution)/shard_map/dot_general | solution.py:79
  402.6 0.1 reshape.184
  402.7 4.0 psum.38
  406.7 0.6 subtract_reduce_fusion
  407.3 39.4 %psum.39 = f32[1024]{0:T(1024)} all-reduce(f32[1024]{0:T(1024)S(1)} %get-tuple-element.4), channel_id=1, replica_groups=mesh['movie'=16,'user'=2] {'movie','user'}, use_global_device_ids=true, to_apply=%region_15.16 | all-reduce | flops 1024 | bytes 8192 | tf_op jit(solution)/shard_map/psum | solution.py:86
  446.7 30.3 %all-reduce.8.cloned.1.call-done = f32[5,1120,1024]{2,1,0:T(8,128)} async-done(((f32[5,1120,1024]{2,1,0:T(8,128)}), f32[5,1120,1024]{2,1,0:T(8,128)}) %all-reduce.8.cloned.1.call-update) | async-done | bytes 22937616 | tf_op jit(solution)/shard_map/psum | solution.py:85
  477.0 16.5 %copy.37 = f32[5,1120,1024]{2,1,0:T(8,128)} copy(f32[5,1120,1024]{2,1,0:T(8,128)} %all-reduce.8.cloned.1.call-done) | data formatting | bytes 45875200
  (27 shorter events, 0.2 us)
Async XLA Ops:
  84.6 33.5 %all-to-all-start.1 = ((s32[16,1,96]{2,1,0:T(1,128)}), s32[16,1,96]{2,1,0:T(1,128)S(1)}, u32[]{:S(2)}, u32[]{:S(2)}) async-start(s32[16,1,96]{2,1,0:T(1,128)} %bitcast.13), calls=%async_computation.1 | async-start | bytes 16384 | tf_op jit(solution)/shard_map/all_to_all | solution.py:54
  92.9 157.8 %all-reduce.4.cloned.1.call-start = ((), (), s32[]{:S(2)}) async-start(), calls=%async_computation.2 | async-start | bytes 524288 | tf_op jit(solution)/shard_map/psum | solution.py:24
  139.1 7.4 %copy-start.1 = (bf16[64,5600]{1,0:T(8,128)(2,1)}, bf16[64,5600]{1,0:T(8,128)(2,1)S(1)}, u32[]{:S(2)}) copy-start(bf16[64,5600]{1,0:T(8,128)(2,1)S(1)} %convert_element_type.42) | copy-start | bytes 2150404
  139.1 7.6 %copy-start.3 = (f32[5,1120]{1,0:T(8,128)S(1)}, f32[5,1120]{1,0:T(8,128)}, u32[]{:S(2)}) copy-start(f32[5,1120]{1,0:T(8,128)} %param.10) | copy-start | bytes 67204
  146.5 239.6 %all-reduce.6.cloned.1.call-start = ((), (), s32[]{:S(2)}) async-start(), calls=%async_computation.3 | async-start | bytes 524288 | tf_op jit(solution)/shard_map/psum | solution.py:24
  147.7 103.0 %copy-start.4 = (f32[1024]{0:T(1024)S(1)}, f32[1024]{0:T(1024)}, u32[]{:S(2)}) copy-start(f32[1024]{0:T(1024)} %param.11) | copy-start | bytes 12292
  149.6 113.3 %slice-start = ((s8[11468800]{0:T(1024)(128)(4,1)}), s8[3080192]{0:T(1024)(128)(4,1)S(1)}, s32[]{:S(2)}) async-start(s8[11468800]{0:T(1024)(128)(4,1)} %bitcast.78), calls=%async_computation.5 | async-start | bytes 6160384
  251.8 11.2 %slice-start.1 = ((s8[11468800]{0:T(1024)(128)(4,1)}), s8[4194304]{0:T(1024)(128)(4,1)S(1)}, s32[]{:S(2)}) async-start(s8[11468800]{0:T(1024)(128)(4,1)} %bitcast.78), calls=%async_computation.6 | async-start | bytes 8388608
  251.8 11.2 %slice-start.2 = ((s8[11468800]{0:T(1024)(128)(4,1)}), s8[4194304]{0:T(1024)(128)(4,1)S(1)}, s32[]{:S(2)}) async-start(s8[11468800]{0:T(1024)(128)(4,1)} %bitcast.78), calls=%async_computation.7 | async-start | bytes 8388608
  279.2 197.9 %all-reduce.8.cloned.1.call-start = ((), (), s32[]{:S(2)}) async-start(), calls=%async_computation.4 | async-start | bytes 45875200 | tf_op jit(solution)/shard_map/psum | solution.py:85
  282.8 3.0 copy-start
  282.8 3.0 copy-start.2
Sparse Core Ops, SparseCore 0:
  146.6 104.0 all-reduce.3
  279.3 106.6 all-reduce.5
  402.7 74.2 all-reduce.7
where the time goes:
time: 501 us; the launch traced here: 500 us
  waiting for transfers between devices  226 us (45%)
  local copies, waits for them, and re-layouts  128 us (26%)
  blocking collectives  57.4 us (11%)
  matrix products  52.3 us (10%)
  between operations  14 us (3%)
  other arithmetic  13.7 us (3%)
  starting transfers between devices  8.78 us (2%)
    psum x2, waiting for transfers between devices, hidden_phase(): all_probs = jax.nn.sigmoid(hid_bias[None, :] + lax.psum(combined, 'movie'))  196 us
    scatter x1, local copies, waits for them, and re-layouts, on_device(): jnp.full((owners, capacity), -1, jnp.int32).at[target, placed]  71.8 us
    psum x1, blocking collectives, on_device(): lax.psum(jnp.sum(positive_own - negative_own, axis=0), ('movie', 'user'))  39.4 us
    psum x1, waiting for transfers between devices, on_device(): weight_grad, visible_grad = lax.psum((weight_grad, visible_grad), 'user')  30.3 us
    scatter x1, local copies, waits for them, and re-layouts, on_device(): jnp.zeros((owners, capacity), jnp.int32).at[target, placed]  25.2 us
    unnamed x17, local copies, waits for them, and re-layouts  16.6 us
    dot_general x1, matrix products, on_device(): lax.dot_general(reconstructed_ratings, negative_group, contract, preferre...  15.5 us
    dot_general x2, matrix products, hidden_phase(): jnp.dot(visible, weight_table, preferred_element_type=jnp.float32)  14.4 us
  transfers between devices with their start and end apart: 4, of which 3 were waited for; matrix products, arithmetic and copies ran while one was open for 8% of the time, Pallas kernels for 0%

commit v1 on v0

--- a/solution.py
+++ b/solution.py
@@ -1,7 +1,354 @@
+import functools
+
 import jax
 import jax.numpy as jnp
 from jax import lax
+from jax.experimental import pallas as pl
+from jax.experimental.pallas import tpu as pltpu
 from jax.sharding import PartitionSpec as P
+
+LANES = 128
+F32 = jnp.float32
+BF16 = jnp.bfloat16
+MIB = 1 << 20
+TILES = (5, 4, 7, 10)
+PARTS = (2, 4, 5, 7)
+SENT = F32
+TN = (((0,), (0,)), ((), ()))
+NT = (((1,), (1,)), ((), ()))
+
+
+def positive_kernel(codes_ref, source, partial_ref, rating_ref, table, shown, movie_s, grade_s, total, arrived):
+    sources, local_users, slots = codes_ref.shape
+    half = slots // 2
+    local_movies = rating_ref.shape[0]
+    columns = source.shape[0]
+    levels = columns // local_movies
+    tile = pick_tile(local_movies, TILES)
+    chunks = row_chunks(columns, arrived.shape[0])
+    copies = [
+        pltpu.make_async_copy(source.at[pl.ds(at, size)], table.at[pl.ds(at, size)], arrived.at[i])
+        for i, (at, size) in enumerate(chunks)
+    ]
+    for copy in copies:
+        copy.start()
+
+    rows = jnp.concatenate([codes_ref[i] for i in range(sources)], axis=0).astype(F32)
+    turned = rows.T
+    both = jnp.concatenate([turned[:half], turned[half:]], axis=1)
+    movie = jnp.floor(both * 0.125)
+    movie_s[...] = movie - (lax.axis_index("movie") * local_movies).astype(F32)
+    grade_s[...] = both - movie * 8.0
+    place = lax.broadcasted_iota(jnp.int32, (tile, LANES), 0).astype(F32).astype(BF16)
+
+    for at in range(0, local_movies, tile):
+
+        def add_slot(slot, found):
+            movie = jnp.broadcast_to(movie_s[pl.ds(slot, 1), :] - float(at), (16, LANES)).astype(BF16)
+            grade = jnp.broadcast_to(grade_s[pl.ds(slot, 1), :], (16, LANES)).astype(BF16)
+            movie = jnp.tile(movie, (tile // 16, 1))
+            grade = jnp.tile(grade, (tile // 16, 1))
+            return jnp.where(place == movie, grade, found)
+
+        found = lax.fori_loop(0, half, add_slot, jnp.full((tile, LANES), -1.0, BF16), unroll=16)
+        wide = found.astype(F32)
+        wide = jnp.maximum(wide, pltpu.roll(wide, LANES // 2, 1))
+        rating_ref[at : at + tile, :] = wide.astype(BF16)
+        for k in range(levels):
+            first = k * local_movies + at
+            shown[first : first + tile, :] = jnp.where(wide == float(k), 1.0, 0.0).astype(BF16)
+
+    for i, (at, size) in enumerate(chunks):
+        copies[i].wait()
+        part = lax.dot_general(shown[at : at + size, :], table[at : at + size, :], TN, preferred_element_type=F32)
+        total[...] = part if i == 0 else total[...] + part
+    for i in range(sources):
+        partial_ref[i] = total[i * local_users : (i + 1) * local_users, :].astype(partial_ref.dtype)
+
+
+def negative_kernel(rows_ref, source, bias_ref, rating_ref, partial_ref, stats_ref, table, probs, total, arrived):
+    sources, local_users, hidden = rows_ref.shape
+    users = sources * local_users
+    local_movies = rating_ref.shape[0]
+    levels = source.shape[0] // local_movies
+    tile = pick_tile(local_movies, TILES)
+    tiles = range(local_movies // tile)
+    block = levels * tile
+    copies = [
+        [
+            pltpu.make_async_copy(
+                source.at[pl.ds(k * local_movies + t * tile, tile)],
+                table.at[pl.ds(t * block + k * tile, tile)],
+                arrived.at[t, k],
+            )
+            for k in range(levels)
+        ]
+        for t in tiles
+    ]
+    for group in copies:
+        for copy in group:
+            copy.start()
+
+    rows = jnp.concatenate([rows_ref[i].astype(F32) for i in range(sources)], axis=0)
+    probs[...] = jnp.concatenate([rows, rows], axis=0).T.astype(BF16)
+    first = lax.broadcasted_iota(jnp.int32, (tile, LANES), 1) < LANES // 2
+
+    def logits(t):
+        for copy in copies[t]:
+            copy.wait()
+        return jnp.dot(table[t * block : (t + 1) * block, :], probs[...], preferred_element_type=F32)
+
+    ready = logits(0)
+    for t in tiles:
+        following = logits(t + 1) if t + 1 < len(tiles) else None
+        own = slice(t * tile, (t + 1) * tile)
+        bias = bias_ref[own, :]
+        level = [ready[k * tile : (k + 1) * tile] + bias[:, k : k + 1] for k in range(levels)]
+        largest = functools.reduce(jnp.maximum, level)
+        level = [jnp.exp(x - largest) for x in level]
+        scale = 1.0 / functools.reduce(jnp.add, level)
+        rating = rating_ref[own, :].astype(F32)
+        scale = jnp.where(rating >= 0.0, scale, 0.0)
+        stats = []
+        for k in range(levels):
+            shown = jnp.where(rating == float(k), 1.0, 0.0)
+            stats.append(jnp.where(first, shown, -(level[k] * scale)).astype(BF16))
+            at = k * local_movies + t * tile
+            stats_ref[at : at + tile, :] = stats[k]
+        stats = jnp.concatenate(stats, axis=0)
+        part = lax.dot_general(
+            stats, table[t * block : (t + 1) * block, :], TN, preferred_element_type=F32
+        )
+        total[...] = part if t == 0 else total[...] + part
+        ready = following
+    for i in range(sources):
+        row = users + i * local_users
+        partial_ref[i] = (-total[row : row + local_users, :]).astype(partial_ref.dtype)
+
+
+def positive_rows_kernel(parts_ref, bias_ref, own_ref, sent_ref):
+    sources = parts_ref.shape[0]
+    summed = functools.reduce(jnp.add, [parts_ref[i].astype(F32) for i in range(sources)])
+    own = jax.nn.sigmoid(bias_ref[...] + summed)
+    own_ref[...] = own
+    low = own.astype(BF16)
+    for i in range(sources):
+        sent_ref[i] = low
+
+
+def negative_rows_kernel(parts_ref, bias_ref, positive_ref, _, sent_ref):
+    sources, local_users, hidden = parts_ref.shape
+    side = 2 * hidden // local_users
+    summed = functools.reduce(jnp.add, [parts_ref[i].astype(F32) for i in range(sources)])
+    own = jax.nn.sigmoid(bias_ref[...] + summed)
+    difference = jnp.sum(positive_ref[...] - own, axis=0, keepdims=True)
+    high = difference.astype(BF16).astype(F32)
+    rest = difference - high
+    pieces = hidden // side
+    split = [x[:, i * side : (i + 1) * side] for x in (high, rest) for i in range(pieces)]
+    low = jnp.concatenate([own, jnp.concatenate(split, axis=0)], axis=1).astype(BF16)
+    for i in range(sources):
+        sent_ref[i] = low
+
+
+def gradient_kernel(stats_a, stats_b, pos_a, pos_b, neg_a, neg_b, target, visible_ref, hidden_ref, lhs, rhs, slots, sent):
+    sources, local_users, hidden = pos_a.shape
+    levels, local_movies, _ = stats_a.shape
+    side = neg_a.shape[2] - hidden
+    pieces = hidden // side
+    buffers, rows, _ = slots.shape
+    parts = local_movies // rows
+    mine = pl.multiple_of(lax.axis_index("user") * LANES, LANES)
+    other = pl.multiple_of(LANES - mine, LANES)
+
+    sides = []
+    for at, pos, neg in ((mine, pos_a, neg_a), (other, pos_b, neg_b)):
+        wide = [neg[i].astype(F32) for i in range(sources)]
+        block = [pos[i].astype(F32) for i in range(sources)] + [x[:, :hidden] for x in wide]
+        rhs[pl.ds(at, LANES), :] = jnp.concatenate(block, axis=0).astype(BF16)
+        sides.append(functools.reduce(jnp.add, [x[:, hidden:] for x in wide]))
+    both = sides[0] + sides[1]
+    both = both[:pieces] + both[pieces:]
+    for i in range(pieces):
+        hidden_ref[:, i * side : (i + 1) * side] = both[i : i + 1]
+    ones = jnp.ones((8, LANES), BF16)
+
+    def send(level, part, slot):
+        place = target.at[level, pl.ds(part * rows, rows)]
+        return pltpu.make_async_copy(slots.at[slot], place, sent.at[slot])
+
+    def one_level(level, carry):
+        a, b = stats_a[level], stats_b[level]
+        lhs[:, pl.ds(mine, LANES)] = a
+        lhs[:, pl.ds(other, LANES)] = b
+        for part in range(parts):
+            count = level * parts + part
+            slot = lax.rem(count, buffers)
+
+            @pl.when(count >= buffers)
+            def _():
+                send(level, part, slot).wait()
+
+            block = lhs[part * rows : (part + 1) * rows, :]
+            slots[slot] = jnp.dot(block, rhs[...], preferred_element_type=F32)
+            send(level, part, slot).start()
+        summed = lax.dot_general(ones, a, NT, preferred_element_type=F32) + lax.dot_general(
+            ones, b, NT, preferred_element_type=F32
+        )
+        visible_ref[pl.ds(level, 1), :] = summed[:1]
+        return carry
+
+    lax.fori_loop(0, levels, one_level, 0)
+    for slot in range(min(buffers, levels * parts)):
+        send(0, 0, slot).wait()
+
+
+def whole(shape):
+    return pl.BlockSpec(shape, lambda *_: (0,) * len(shape))
+
+
+def params(limit):
+    return pltpu.CompilerParams(vmem_limit_bytes=limit)
+
+
+def exchange(x):
+    return lax.all_to_all(x, "movie", split_axis=0, concat_axis=0, tiled=True)
+
+
+def pick_tile(local_movies, parts):
+    for count in parts:
+        if local_movies % count == 0 and (local_movies // count) % 16 == 0:
+            return local_movies // count
+    return None
+
+
+def row_chunks(rows, count):
+    blocks = pl.cdiv(rows, 256)
+    edges = [min(rows, 256 * (blocks * i // count)) for i in range(count)] + [rows]
+    return [(a, b - a) for a, b in zip(edges, edges[1:])]
+
+
+def on_device_kernels(movie_ids, ratings, valid, weights, vis_bias, hid_bias):
+    owners = lax.axis_size("movie")
+    local_users, slots = movie_ids.shape
+    levels, local_movies, hidden = weights.shape
+    columns = levels * local_movies
+    users = owners * local_users
+    tile = pick_tile(local_movies, TILES)
+    rows = pick_tile(local_movies, PARTS)
+    swap = [(0, 1), (1, 0)]
+    matmul = 2 * users * columns * hidden
+    table_bytes = weights.size * 2
+
+    code = jnp.where(valid == 1, movie_ids * 8 + ratings, -8)
+    codes = exchange(jnp.broadcast_to(code[None], (owners, local_users, slots)))
+    table = pltpu.with_memory_space_constraint(weights.reshape(columns, hidden), pltpu.HBM)
+    vis_rows = vis_bias.T
+    bias_row = hid_bias[None, :]
+    table_scratch = pltpu.VMEM((columns, hidden), BF16)
+    total_scratch = pltpu.VMEM((LANES, hidden), F32)
+    vmem = pl.BlockSpec(memory_space=pltpu.VMEM)
+    table_spec = pl.BlockSpec(memory_space=pltpu.HBM)
+    parts_shape = (owners, local_users, hidden)
+
+    positive_part, rating = pl.pallas_call(
+        positive_kernel,
+        in_specs=[vmem, table_spec],
+        out_specs=[vmem, vmem],
+        out_shape=[
+            jax.ShapeDtypeStruct(parts_shape, SENT),
+            jax.ShapeDtypeStruct((local_movies, LANES), BF16),
+        ],
+        scratch_shapes=[
+            table_scratch,
+            pltpu.VMEM((columns, LANES), BF16),
+            pltpu.VMEM((slots // 2, LANES), F32),
+            pltpu.VMEM((slots // 2, LANES), F32),
+            total_scratch,
+            pltpu.SemaphoreType.DMA((4,)),
+        ],
+        compiler_params=params(32 * MIB),
+        cost_estimate=pl.CostEstimate(flops=matmul, bytes_accessed=table_bytes, transcendentals=0),
+        name="positive",
+    )(codes, table)
+
+    positive_own, sent = pl.pallas_call(
+        positive_rows_kernel,
+        out_shape=[
+            jax.ShapeDtypeStruct((local_users, hidden), F32),
+            jax.ShapeDtypeStruct(parts_shape, BF16),
+        ],
+        compiler_params=params(8 * MIB),
+        name="positive_rows",
+    )(exchange(positive_part), bias_row)
+    pos_a = exchange(sent)
+    pos_b = lax.ppermute(pos_a, "user", swap)
+
+    negative_part, stats_a = pl.pallas_call(
+        negative_kernel,
+        in_specs=[vmem, table_spec, vmem, vmem],
+        out_specs=[vmem, vmem],
+        out_shape=[
+            jax.ShapeDtypeStruct(parts_shape, SENT),
+            jax.ShapeDtypeStruct((columns, LANES), BF16),
+        ],
+        scratch_shapes=[
+            table_scratch,
+            pltpu.VMEM((hidden, LANES), BF16),
+            total_scratch,
+            pltpu.SemaphoreType.DMA((local_movies // tile, levels)),
+        ],
+        compiler_params=params(32 * MIB),
+        cost_estimate=pl.CostEstimate(flops=2 * matmul, bytes_accessed=table_bytes, transcendentals=0),
+        name="negative",
+    )(pos_a, table, vis_rows, rating)
+    stats_a = stats_a.reshape(levels, local_movies, LANES)
+    stats_b = lax.ppermute(stats_a, "user", swap)
+
+    sent = pl.pallas_call(
+        negative_rows_kernel,
+        in_specs=[vmem, vmem, vmem, pl.BlockSpec(memory_space=pl.ANY)],
+        out_shape=jax.ShapeDtypeStruct((owners, local_users, hidden + 2 * hidden // local_users), BF16),
+        compiler_params=params(8 * MIB),
+        name="negative_rows",
+    )(exchange(negative_part), bias_row, positive_own, pos_b)
+    neg_a = exchange(sent)
+    neg_b = lax.ppermute(neg_a, "user", swap)
+
+    weight_grad, visible_grad, hidden_grad = pl.pallas_call(
+        gradient_kernel,
+        in_specs=[vmem] * 6,
+        out_specs=[pl.BlockSpec(memory_space=pltpu.HBM), vmem, vmem],
+        out_shape=[
+            jax.ShapeDtypeStruct(weights.shape, F32),
+            jax.ShapeDtypeStruct((levels, local_movies), F32),
+            jax.ShapeDtypeStruct((1, hidden), F32),
+        ],
+        scratch_shapes=[
+            pltpu.VMEM((local_movies, 2 * LANES), BF16),
+            pltpu.VMEM((2 * LANES, hidden), BF16),
+            pltpu.VMEM((3, rows, hidden), F32),
+            pltpu.SemaphoreType.DMA((3,)),
+        ],
+        compiler_params=params(32 * MIB),
+        cost_estimate=pl.CostEstimate(flops=4 * matmul, bytes_accessed=2 * table_bytes, transcendentals=0),
+        name="gradient",
+    )(stats_a, stats_b, pos_a, pos_b, neg_a, neg_b)
+    return weight_grad, visible_grad, hidden_grad[0], positive_own
+
+
+def fits_kernels(mesh, local_users, slots, levels, local_movies, hidden):
+    users = mesh.shape["movie"] * local_users
+    return (
+        mesh.shape["user"] == 2
+        and users == LANES // 2
+        and slots % 16 == 0
+        and hidden % (LANES * local_users) == 0
+        and local_users == 4
+        and levels < 8
+        and pick_tile(local_movies, TILES) is not None
+        and pick_tile(local_movies, PARTS) is not None
+    )
 
 
 def reconstruct(hidden_rows, weight_table, bias_row, rated_mask, levels):
@@ -102,6 +449,18 @@
         P(),
     )
     out_specs = (P(None, "movie", None), P(None, "movie"), P(), P(("movie", "user"), None))
-    return jax.shard_map(
-        on_device, mesh=mesh, in_specs=in_specs, out_specs=out_specs, check_vma=False
-    )
+
+    def step(movie_ids, ratings, valid, weights, vis_bias, hid_bias):
+        owners = mesh.shape["movie"]
+        local_users = movie_ids.shape[0] // (owners * mesh.shape["user"])
+        levels, movies, hidden = weights.shape
+        fits = fits_kernels(mesh, local_users, movie_ids.shape[1], levels, movies // owners, hidden)
+        return jax.shard_map(
+            on_device_kernels if fits else on_device,
+            mesh=mesh,
+            in_specs=in_specs,
+            out_specs=out_specs,
+            check_vma=False,
+        )(movie_ids, ratings, valid, weights, vis_bias, hid_bias)
+
+    return step

time: 501 us -> 91.9 us (0.18)
  waiting for transfers between devices: 226 us -> 19.1 us
  local copies, waits for them, and re-layouts: 128 us -> 0.26 us
  matrix products: 52.3 us -> 0 us
  Pallas kernels: 0 us -> 24.5 us
  blocking collectives: 57.4 us -> 38.1 us
  between operations: 14 us -> 0.71 us
  other arithmetic: 13.7 us -> 0.73 us
    psum x3 -> x0, waiting for transfers between devices: 226 us -> none  [the longest x2 196 us: hidden_phase(): all_probs = jax.nn.sigmoid(hid_bias[None, :] + lax.psum(combined, 'movie'))]
    scatter x2 -> x0, local copies, waits for them, and re-layouts: 97 us -> none  [the longest x1 71.8 us: on_device(): jnp.full((owners, capacity), -1, jnp.int32).at[target, placed]]
    dot_general x6 -> x0, matrix products: 52.3 us -> none  [the longest x1 15.5 us: on_device(): lax.dot_general(reconstructed_ratings, negative_group, contract, preferre...]
    psum x2 -> x0, blocking collectives: 43.4 us -> none  [the longest x1 39.4 us: on_device(): lax.psum(jnp.sum(positive_own - negative_own, axis=0), ('movie', 'user'))]
    pallas_call x0 -> x5, Pallas kernels: none -> 24.5 us  [the longest x1 10.5 us: on_device_kernels(): pl.pallas_call(gradient_kernel, in_specs=[vmem] * 6, out_specs=[pl.BlockS...]
    all_to_all x1 -> x3, blocking collectives: 14 us -> 38.1 us  [exchange(): return lax.all_to_all(x, 'movie', split_axis=0, concat_axis=0, tiled=True)]
    all_to_all x1 -> x2, waiting for transfers between devices: 0.01 us -> 16.7 us  [exchange(): return lax.all_to_all(x, 'movie', split_axis=0, concat_axis=0, tiled=True)]
    unnamed x17 -> x7, local copies, waits for them, and re-layouts: 16.6 us -> 0.25 us
  transfers between devices with their start and end apart: 4 -> 5, of which waited for: 3 -> 4; matrix products, arithmetic and copies ran while one was open for 8% -> 0% of each run, Pallas kernels for 0% -> 0%
where the time goes in v1:
time: 91.9 us; the launch traced here: 91.4 us
  blocking collectives  38.1 us (41%)
  Pallas kernels  24.5 us (27%)
  waiting for transfers between devices  19.1 us (21%)
  starting transfers between devices  8 us (9%)
    all_to_all x3, blocking collectives, exchange(): return lax.all_to_all(x, 'movie', split_axis=0, concat_axis=0, tiled=True)  38.1 us
    all_to_all x2, waiting for transfers between devices, exchange(): return lax.all_to_all(x, 'movie', split_axis=0, concat_axis=0, tiled=True)  16.7 us
    pallas_call x1, Pallas kernels, on_device_kernels(): pl.pallas_call(gradient_kernel, in_specs=[vmem] * 6, out_specs=[pl.BlockS...  10.5 us
    pallas_call x1, Pallas kernels, on_device_kernels(): pl.pallas_call(negative_kernel, in_specs=[vmem, table_spec, vmem, vmem],...  8.26 us
    all_to_all x2, starting transfers between devices, exchange(): return lax.all_to_all(x, 'movie', split_axis=0, concat_axis=0, tiled=True)  7.38 us
    pallas_call x1, Pallas kernels, on_device_kernels(): pl.pallas_call(positive_kernel, in_specs=[vmem, table_spec], out_specs=[v...  5 us
  transfers between devices with their start and end apart: 5, of which 4 were waited for; matrix products, arithmetic and copies ran while one was open for 0% of the time, Pallas kernels for 0%

profile of v1, /device:TPU:0, one launch (start us, length us, event | category | flops | bytes accessed | tf_op | source)
XLA Modules:
  0.0 91.4 jit_solution(17058093183366056446)
XLA Ops:
  0.6 0.0 copy-start
  0.6 0.0 copy-start.2
  0.7 0.7 add_select_fusion
  1.4 15.5 %all_to_all.25.codes_ref = s32[16,4,128]{2,1,0:T(4,128)S(1)} all-to-all(s32[16,4,128]{2,1,0:T(4,128)S(1)} %broadcast_in_dim.14), channel_id=1, replica_groups=mesh['movie'=16,'user'=2] {'movie'}, dimensions={0} | all-to-all | bytes 65536 | tf_op jit(solution)/shard_map/all_to_all | solution.py:215
  16.9 5.0 %positive.1 = (f32[16,4,1024]{2,1,0:T(4,128)S(1)}, bf16[1120,128]{1,0:T(8,128)(2,1)S(1)}) custom-call(s32[16,4,128]{2,1,0:T(4,128)S(1)} %all_to_all.25.codes_ref, bf16[5600,1024]{1,0:T(8,128)(2,1)} %bitcast.10), custom_call_target="tpu_custom_call" | custom-call | flops 734003200 | bytes 11468800 | tf_op jit(solution)/shard_map/positive/pallas_call | solution.py:254
  21.9 11.1 %all_to_all.26.parts_ref = f32[16,4,1024]{2,1,0:T(4,128)S(1)} all-to-all(f32[16,4,1024]{2,1,0:T(4,128)S(1)} %get-tuple-element.13), channel_id=1, replica_groups=mesh['movie'=16,'user'=2] {'movie'}, dimensions={0} | all-to-all | bytes 524288 | tf_op jit(solution)/shard_map/all_to_all | solution.py:215
  33.0 0.0 copy-done
  33.1 0.7 positive_rows.1
  33.8 0.0 copy-start.1
  33.8 3.8 %all-to-all-start.2 = ((bf16[16,4,1024]{2,1,0:T(4,128)(2,1)}), bf16[16,4,1024]{2,1,0:T(4,128)(2,1)S(1)}, u32[]{:S(2)}, u32[]{:S(2)}) async-start(bf16[16,4,1024]{2,1,0:T(4,128)(2,1)} %get-tuple-element.14), calls=%async_computation.2 | async-start | bytes 262144 | tf_op jit(solution)/shard_map/all_to_all | solution.py:215
  37.6 0.0 copy-done.2
  37.6 0.2 copy.10
  37.9 7.5 %all-to-all-done.2.rows_ref.pos_a = bf16[16,4,1024]{2,1,0:T(4,128)(2,1)S(1)} async-done(((bf16[16,4,1024]{2,1,0:T(4,128)(2,1)}), bf16[16,4,1024]{2,1,0:T(4,128)(2,1)S(1)}, u32[]{:S(2)}, u32[]{:S(2)}) %all-to-all-start.2) | async-done | bytes 131104 | tf_op jit(solution)/shard_map/all_to_all | solution.py:215
  45.4 8.3 %negative.1 = (f32[16,4,1024]{2,1,0:T(4,128)}, bf16[5600,128]{1,0:T(8,128)(2,1)S(1)}) custom-call(bf16[16,4,1024]{2,1,0:T(4,128)(2,1)S(1)} %all-to-all-done.2.rows_ref.pos_a, bf16[5600,1024]{1,0:T(8,128)(2,1)} %bitcast.11, f32[1120,5]{1,0:T(8,128)S(1)} %bitcast.5, bf16[1120,128]{1,0:T(8,128)(2,1)S(1)} %get-tuple-element.15.rating_ref), custom_call_target="tpu_custom_call" | custom-call | flops 1468006400 | bytes 11468800 | tf_op jit(solution)/shard_map/negative/pallas_call | solution.py:287
  53.7 0.1 collective-permute-start
  53.7 3.5 %all-to-all-start.3 = ((f32[16,4,1024]{2,1,0:T(4,128)}), f32[16,4,1024]{2,1,0:T(4,128)S(1)}, u32[]{:S(2)}, u32[]{:S(2)}) async-start(f32[16,4,1024]{2,1,0:T(4,128)} %get-tuple-element.17), calls=%async_computation.3 | async-start | bytes 524288 | tf_op jit(solution)/shard_map/all_to_all | solution.py:215
  57.3 0.5 collective-permute-start.1
  57.8 1.0 %collective-permute-done.1._.pos_b = bf16[16,4,1024]{2,1,0:T(4,128)(2,1)S(1)} collective-permute-done((bf16[16,4,1024]{2,1,0:T(4,128)(2,1)S(1)}, bf16[16,4,1024]{2,1,0:T(4,128)(2,1)S(1)}, u32[]{:S(2)}, u32[]{:S(2)}) %collective-permute-start.1) | collective-permute-done | bytes 131104 | tf_op jit(solution)/shard_map/ppermute | solution.py:285
  58.8 9.2 %all-to-all-done.3.parts_ref = f32[16,4,1024]{2,1,0:T(4,128)S(1)} async-done(((f32[16,4,1024]{2,1,0:T(4,128)}), f32[16,4,1024]{2,1,0:T(4,128)S(1)}, u32[]{:S(2)}, u32[]{:S(2)}) %all-to-all-start.3) | async-done | bytes 262176 | tf_op jit(solution)/shard_map/all_to_all | solution.py:215
  68.0 0.0 copy-done.1
  68.0 0.1 negative_rows.1
  68.0 11.4 %all_to_all.27.neg_a = bf16[16,4,1536]{2,1,0:T(4,128)(2,1)S(1)} all-to-all(bf16[16,4,1536]{2,1,0:T(4,128)(2,1)S(1)} %negative_rows.1), channel_id=1, replica_groups=mesh['movie'=16,'user'=2] {'movie'}, dimensions={0} | all-to-all | bytes 393216 | tf_op jit(solution)/shard_map/all_to_all | solution.py:215
  79.5 0.0 collective-permute-start.2
  79.5 1.4 %collective-permute-done.2.neg_b = bf16[16,4,1536]{2,1,0:T(4,128)(2,1)S(1)} collective-permute-done((bf16[16,4,1536]{2,1,0:T(4,128)(2,1)S(1)}, bf16[16,4,1536]{2,1,0:T(4,128)(2,1)S(1)}, u32[]{:S(2)}, u32[]{:S(2)}) %collective-permute-start.2) | collective-permute-done | bytes 196640 | tf_op jit(solution)/shard_map/ppermute | solution.py:316
  80.9 0.0 collective-permute-done.stats_b
  80.9 10.5 %gradient.1 = (f32[5,1120,1024]{2,1,0:T(8,128)}, f32[5,1120]{1,0:T(8,128)}, f32[1,1024]{1,0:T(1,128)}) custom-call(bf16[5,1120,128]{2,1,0:T(8,128)(2,1)S(1)} %bitcast.9, bf16[5,1120,128]{2,1,0:T(8,128)(2,1)} %collective-permute-done.stats_b, bf16[16,4,1024]{2,1,0:T(4,128)(2,1)S(1)} %all-to-all-done.2.rows_ref.pos_a, ...), custom_call_target="tpu_custom_call" | custom-call | flops 2936012800 | bytes 22937600 | tf_op jit(solution)/shard_map/gradient/pallas_call | solution.py:318
  (1 shorter events, 0.0 us)
Async XLA Ops:
  0.6 32.4 %copy-start = (f32[1024]{0:T(1024)S(1)}, f32[1024]{0:T(1024)}, u32[]{:S(2)}) copy-start(f32[1024]{0:T(1024)} %param.11) | copy-start | bytes 12292
  0.6 37.0 %copy-start.2 = (f32[5,1120]{1,0:T(8,128)S(1)}, f32[5,1120]{1,0:T(8,128)}, u32[]{:S(2)}) copy-start(f32[5,1120]{1,0:T(8,128)} %param.10) | copy-start | bytes 67204
  33.8 34.2 %copy-start.1 = (f32[4,1024]{1,0:T(4,128)S(1)}, f32[4,1024]{1,0:T(4,128)}, u32[]{:S(2)}) copy-start(f32[4,1024]{1,0:T(4,128)} %get-tuple-element.12.positive_ref) | copy-start | bytes 49156
  33.8 11.6 %all-to-all-start.2 = ((bf16[16,4,1024]{2,1,0:T(4,128)(2,1)}), bf16[16,4,1024]{2,1,0:T(4,128)(2,1)S(1)}, u32[]{:S(2)}, u32[]{:S(2)}) async-start(bf16[16,4,1024]{2,1,0:T(4,128)(2,1)} %get-tuple-element.14), calls=%async_computation.2 | async-start | bytes 262144 | tf_op jit(solution)/shard_map/all_to_all | solution.py:215
  53.7 27.3 %collective-permute-start = (bf16[5,1120,128]{2,1,0:T(8,128)(2,1)S(1)}, bf16[5,1120,128]{2,1,0:T(8,128)(2,1)}, u32[]{:S(2)}, u32[]{:S(2)}) collective-permute-start(bf16[5,1120,128]{2,1,0:T(8,128)(2,1)S(1)} %bitcast.8), channel_id=1, source_target_pairs={{0,1},{1,0},{2,3},{3,2},{4,5},{5,4},{6,7},{7,6},{8,9},{9,8},{10,11... | collective-permute-start | bytes 4300808 | tf_op jit(solution)/shard_map/ppermute | solution.py:306
  53.7 14.3 %all-to-all-start.3 = ((f32[16,4,1024]{2,1,0:T(4,128)}), f32[16,4,1024]{2,1,0:T(4,128)S(1)}, u32[]{:S(2)}, u32[]{:S(2)}) async-start(f32[16,4,1024]{2,1,0:T(4,128)} %get-tuple-element.17), calls=%async_computation.3 | async-start | bytes 524288 | tf_op jit(solution)/shard_map/all_to_all | solution.py:215
  57.3 1.5 %collective-permute-start.1 = (bf16[16,4,1024]{2,1,0:T(4,128)(2,1)S(1)}, bf16[16,4,1024]{2,1,0:T(4,128)(2,1)S(1)}, u32[]{:S(2)}, u32[]{:S(2)}) collective-permute-start(bf16[16,4,1024]{2,1,0:T(4,128)(2,1)S(1)} %all-to-all-done.2.rows_ref.pos_a), channel_id=1, source_target_pairs={{0,1},{1,0},{2,3},{3,2},{4,5},{5,4},{6,7},{7,6},{8,9},{9,8},{10,11... | collective-permute-start | bytes 393224 | tf_op jit(solution)/shard_map/ppermute | solution.py:285
  79.5 1.4 %collective-permute-start.2 = (bf16[16,4,1536]{2,1,0:T(4,128)(2,1)S(1)}, bf16[16,4,1536]{2,1,0:T(4,128)(2,1)S(1)}, u32[]{:S(2)}, u32[]{:S(2)}) collective-permute-start(bf16[16,4,1536]{2,1,0:T(4,128)(2,1)S(1)} %all_to_all.27.neg_a), channel_id=1, source_target_pairs={{0,1},{1,0},{2,3},{3,2},{4,5},{5,4},{6,7},{7,6},{8,9},{9,8},{10,11... | collective-permute-start | bytes 589832 | tf_op jit(solution)/shard_map/ppermute | solution.py:316

commit v2 on v1

--- a/solution.py
+++ b/solution.py
@@ -11,25 +11,30 @@
 F32 = jnp.float32
 BF16 = jnp.bfloat16
 MIB = 1 << 20
-TILES = (5, 4, 7, 10)
+TILES = (7, 5, 4, 10)
 PARTS = (2, 4, 5, 7)
-SENT = F32
+WIDE_TILE = 256
 TN = (((0,), (0,)), ((), ()))
 NT = (((1,), (1,)), ((), ()))
 
 
-def positive_kernel(codes_ref, source, partial_ref, rating_ref, table, shown, movie_s, grade_s, total, arrived):
+def positive_kernel(codes_ref, source, partial_ref, rating_ref, head, table, shown, movie_s, grade_s, total, arrived):
     sources, local_users, slots = codes_ref.shape
     half = slots // 2
     local_movies = rating_ref.shape[0]
-    columns = source.shape[0]
-    levels = columns // local_movies
-    tile = pick_tile(local_movies, TILES)
-    chunks = row_chunks(columns, arrived.shape[0])
-    copies = [
-        pltpu.make_async_copy(source.at[pl.ds(at, size)], table.at[pl.ds(at, size)], arrived.at[i])
-        for i, (at, size) in enumerate(chunks)
-    ]
+    levels = source.shape[0] // local_movies
+    tile = head.shape[0] // levels
+    rest = local_movies - tile
+    blocks = [(0, levels * tile, head, 0)]
+    blocks += [(levels * tile + k * rest, rest, table, k * rest) for k in range(levels)]
+    copies = []
+    for k in range(levels):
+        first = k * local_movies
+        copies.append((source.at[pl.ds(first, tile)], head.at[pl.ds(k * tile, tile)]))
+    for k in range(levels):
+        first = k * local_movies + tile
+        copies.append((source.at[pl.ds(first, rest)], table.at[pl.ds(k * rest, rest)]))
+    copies = [pltpu.make_async_copy(*pair, arrived.at[i]) for i, pair in enumerate(copies)]
     for copy in copies:
         copy.start()
 
@@ -55,54 +60,64 @@
         wide = jnp.maximum(wide, pltpu.roll(wide, LANES // 2, 1))
         rating_ref[at : at + tile, :] = wide.astype(BF16)
         for k in range(levels):
-            first = k * local_movies + at
+            first = k * tile if at == 0 else levels * tile + k * rest + at - tile
             shown[first : first + tile, :] = jnp.where(wide == float(k), 1.0, 0.0).astype(BF16)
 
-    for i, (at, size) in enumerate(chunks):
-        copies[i].wait()
-        part = lax.dot_general(shown[at : at + size, :], table[at : at + size, :], TN, preferred_element_type=F32)
+    waits = [copies[:levels]] + [[copy] for copy in copies[levels:]]
+    for i, (at, size, ref, start) in enumerate(blocks):
+        for copy in waits[i]:
+            copy.wait()
+        part = lax.dot_general(
+            shown[at : at + size, :], ref[start : start + size, :], TN, preferred_element_type=F32
+        )
         total[...] = part if i == 0 else total[...] + part
     for i in range(sources):
         partial_ref[i] = total[i * local_users : (i + 1) * local_users, :].astype(partial_ref.dtype)
 
 
-def negative_kernel(rows_ref, source, bias_ref, rating_ref, partial_ref, stats_ref, table, probs, total, arrived):
+def negative_kernel(rows_ref, source, head, bias_ref, rating_ref, own_ref, partial_ref, stats_ref, own_out, table, probs, bias_s, total, arrived, sent):
     sources, local_users, hidden = rows_ref.shape
     users = sources * local_users
     local_movies = rating_ref.shape[0]
     levels = source.shape[0] // local_movies
-    tile = pick_tile(local_movies, TILES)
-    tiles = range(local_movies // tile)
-    block = levels * tile
-    copies = [
+    held = head.shape[0] // levels
+    tiles = movie_tiles(held, local_movies)
+    copies = [[]] + [
         [
             pltpu.make_async_copy(
-                source.at[pl.ds(k * local_movies + t * tile, tile)],
-                table.at[pl.ds(t * block + k * tile, tile)],
+                source.at[pl.ds(k * local_movies + at, tile)],
+                table.at[pl.ds(levels * (at - held) + k * tile, tile)],
                 arrived.at[t, k],
             )
             for k in range(levels)
         ]
-        for t in tiles
+        for t, (at, tile) in enumerate(tiles[1:])
     ]
     for group in copies:
         for copy in group:
             copy.start()
 
+    own_copy = pltpu.make_async_copy(own_ref, own_out, sent)
+    own_copy.start()
+    spare = jnp.zeros((8 - levels, local_movies), F32)
+    bias_s[...] = jnp.concatenate([bias_ref[...], spare], axis=0).T
     rows = jnp.concatenate([rows_ref[i].astype(F32) for i in range(sources)], axis=0)
     probs[...] = jnp.concatenate([rows, rows], axis=0).T.astype(BF16)
-    first = lax.broadcasted_iota(jnp.int32, (tile, LANES), 1) < LANES // 2
+    def block(t):
+        at, tile = tiles[t]
+        return head[...] if t == 0 else table[levels * (at - held) : levels * (at - held + tile), :]
 
     def logits(t):
         for copy in copies[t]:
             copy.wait()
-        return jnp.dot(table[t * block : (t + 1) * block, :], probs[...], preferred_element_type=F32)
+        return jnp.dot(block(t), probs[...], preferred_element_type=F32)
 
     ready = logits(0)
-    for t in tiles:
+    for t, (start, tile) in enumerate(tiles):
         following = logits(t + 1) if t + 1 < len(tiles) else None
-        own = slice(t * tile, (t + 1) * tile)
-        bias = bias_ref[own, :]
+        first = lax.broadcasted_iota(jnp.int32, (tile, LANES), 1) < LANES // 2
+        own = slice(start, start + tile)
+        bias = bias_s[own, :]
         level = [ready[k * tile : (k + 1) * tile] + bias[:, k : k + 1] for k in range(levels)]
         largest = functools.reduce(jnp.maximum, level)
         level = [jnp.exp(x - largest) for x in level]
@@ -113,17 +128,18 @@
         for k in range(levels):
             shown = jnp.where(rating == float(k), 1.0, 0.0)
             stats.append(jnp.where(first, shown, -(level[k] * scale)).astype(BF16))
-            at = k * local_movies + t * tile
+            at = k * local_movies + start
             stats_ref[at : at + tile, :] = stats[k]
         stats = jnp.concatenate(stats, axis=0)
         part = lax.dot_general(
-            stats, table[t * block : (t + 1) * block, :], TN, preferred_element_type=F32
+            stats, block(t), TN, preferred_element_type=F32
         )
         total[...] = part if t == 0 else total[...] + part
         ready = following
     for i in range(sources):
         row = users + i * local_users
         partial_ref[i] = (-total[row : row + local_users, :]).astype(partial_ref.dtype)
+    own_copy.wait()
 
 
 def positive_rows_kernel(parts_ref, bias_ref, own_ref, sent_ref):
@@ -136,7 +152,7 @@
         sent_ref[i] = low
 
 
-def negative_rows_kernel(parts_ref, bias_ref, positive_ref, _, sent_ref):
+def negative_rows_kernel(parts_ref, bias_ref, positive_ref, sent_ref):
     sources, local_users, hidden = parts_ref.shape
     side = 2 * hidden // local_users
     summed = functools.reduce(jnp.add, [parts_ref[i].astype(F32) for i in range(sources)])
@@ -151,26 +167,36 @@
         sent_ref[i] = low
 
 
-def gradient_kernel(stats_a, stats_b, pos_a, pos_b, neg_a, neg_b, target, visible_ref, hidden_ref, lhs, rhs, slots, sent):
-    sources, local_users, hidden = pos_a.shape
+def gathered_rows_kernel(pos_ref, neg_ref, rows_ref):
+    sources, _, hidden = pos_ref.shape
+    wide = [neg_ref[i].astype(F32) for i in range(sources)]
+    block = [pos_ref[i].astype(F32) for i in range(sources)] + [x[:, :hidden] for x in wide]
+    sides = functools.reduce(jnp.add, [x[:, hidden:] for x in wide])
+    pieces = sides.shape[0] // 2
+    sides = sides[:pieces] + sides[pieces:]
+    rest = jnp.concatenate([sides[i : i + 1] for i in range(pieces)], axis=1)
+    terms = []
+    for _ in range(3):
+        terms.append(rest.astype(BF16).astype(F32))
+        rest = rest - terms[-1]
+    spare = jnp.zeros((rows_ref.shape[0] - LANES - len(terms), hidden), F32)
+    rows_ref[...] = jnp.concatenate(block + terms + [spare], axis=0).astype(BF16)
+
+
+def gradient_kernel(stats_a, stats_b, rows_a, rows_b, target, visible_out, hidden_out, stats_s, visible_ref, hidden_ref, lhs, rhs, slots, sent, got, done):
     levels, local_movies, _ = stats_a.shape
-    side = neg_a.shape[2] - hidden
-    pieces = hidden // side
     buffers, rows, _ = slots.shape
     parts = local_movies // rows
     mine = pl.multiple_of(lax.axis_index("user") * LANES, LANES)
     other = pl.multiple_of(LANES - mine, LANES)
 
-    sides = []
-    for at, pos, neg in ((mine, pos_a, neg_a), (other, pos_b, neg_b)):
-        wide = [neg[i].astype(F32) for i in range(sources)]
-        block = [pos[i].astype(F32) for i in range(sources)] + [x[:, :hidden] for x in wide]
-        rhs[pl.ds(at, LANES), :] = jnp.concatenate(block, axis=0).astype(BF16)
-        sides.append(functools.reduce(jnp.add, [x[:, hidden:] for x in wide]))
-    both = sides[0] + sides[1]
-    both = both[:pieces] + both[pieces:]
-    for i in range(pieces):
-        hidden_ref[:, i * side : (i + 1) * side] = both[i : i + 1]
+    fetch = [pltpu.make_async_copy(stats_b.at[i], stats_s.at[i], got.at[i]) for i in range(levels)]
+    for copy in fetch:
+        copy.start()
+    rhs[pl.ds(mine, LANES), :] = rows_a[:LANES, :]
+    rhs[pl.ds(other, LANES), :] = rows_b[:LANES, :]
+    sums = [jnp.sum(ref[LANES:, :].astype(F32), axis=0, keepdims=True) for ref in (rows_a, rows_b)]
+    hidden_ref[...] = sums[0] + sums[1]
     ones = jnp.ones((8, LANES), BF16)
 
     def send(level, part, slot):
@@ -178,7 +204,8 @@
         return pltpu.make_async_copy(slots.at[slot], place, sent.at[slot])
 
     def one_level(level, carry):
-        a, b = stats_a[level], stats_b[level]
+        pltpu.make_async_copy(stats_b.at[level], stats_s.at[level], got.at[level]).wait()
+        a, b = stats_a[level], stats_s[level]
         lhs[:, pl.ds(mine, LANES)] = a
         lhs[:, pl.ds(other, LANES)] = b
         for part in range(parts):
@@ -199,8 +226,16 @@
         return carry
 
     lax.fori_loop(0, levels, one_level, 0)
+    small = [
+        pltpu.make_async_copy(visible_ref, visible_out, done.at[0]),
+        pltpu.make_async_copy(hidden_ref, hidden_out, done.at[1]),
+    ]
+    for copy in small:
+        copy.start()
     for slot in range(min(buffers, levels * parts)):
         send(0, 0, slot).wait()
+    for copy in small:
+        copy.wait()
 
 
 def whole(shape):
@@ -222,10 +257,11 @@
     return None
 
 
-def row_chunks(rows, count):
-    blocks = pl.cdiv(rows, 256)
-    edges = [min(rows, 256 * (blocks * i // count)) for i in range(count)] + [rows]
-    return [(a, b - a) for a, b in zip(edges, edges[1:])]
+def movie_tiles(held, movies):
+    wide, left = divmod(movies - held, WIDE_TILE)
+    sizes = [held] + [WIDE_TILE] * wide
+    sizes += [left // 2] * 2 if left and left % 32 == 0 else [left] * (left > 0)
+    return [(sum(sizes[:i]), size) for i, size in enumerate(sizes)]
 
 
 def on_device_kernels(movie_ids, ratings, valid, weights, vis_bias, hid_bias):
@@ -235,7 +271,7 @@
     columns = levels * local_movies
     users = owners * local_users
     tile = pick_tile(local_movies, TILES)
-    rows = pick_tile(local_movies, PARTS)
+    part = pick_tile(local_movies, PARTS)
     swap = [(0, 1), (1, 0)]
     matmul = 2 * users * columns * hidden
     table_bytes = weights.size * 2
@@ -243,21 +279,21 @@
     code = jnp.where(valid == 1, movie_ids * 8 + ratings, -8)
     codes = exchange(jnp.broadcast_to(code[None], (owners, local_users, slots)))
     table = pltpu.with_memory_space_constraint(weights.reshape(columns, hidden), pltpu.HBM)
-    vis_rows = vis_bias.T
     bias_row = hid_bias[None, :]
-    table_scratch = pltpu.VMEM((columns, hidden), BF16)
+    table_scratch = pltpu.VMEM((levels * (local_movies - tile), hidden), BF16)
     total_scratch = pltpu.VMEM((LANES, hidden), F32)
     vmem = pl.BlockSpec(memory_space=pltpu.VMEM)
     table_spec = pl.BlockSpec(memory_space=pltpu.HBM)
     parts_shape = (owners, local_users, hidden)
 
-    positive_part, rating = pl.pallas_call(
+    positive_part, rating, head = pl.pallas_call(
         positive_kernel,
         in_specs=[vmem, table_spec],
-        out_specs=[vmem, vmem],
+        out_specs=[vmem, vmem, vmem],
         out_shape=[
-            jax.ShapeDtypeStruct(parts_shape, SENT),
+            pltpu.VMEM(parts_shape, F32),
             jax.ShapeDtypeStruct((local_movies, LANES), BF16),
+            pltpu.VMEM((levels * tile, hidden), BF16),
         ],
         scratch_shapes=[
             table_scratch,
@@ -265,7 +301,7 @@
             pltpu.VMEM((slots // 2, LANES), F32),
             pltpu.VMEM((slots // 2, LANES), F32),
             total_scratch,
-            pltpu.SemaphoreType.DMA((4,)),
+            pltpu.SemaphoreType.DMA((2 * levels,)),
         ],
         compiler_params=params(32 * MIB),
         cost_estimate=pl.CostEstimate(flops=matmul, bytes_accessed=table_bytes, transcendentals=0),
@@ -275,66 +311,76 @@
     positive_own, sent = pl.pallas_call(
         positive_rows_kernel,
         out_shape=[
-            jax.ShapeDtypeStruct((local_users, hidden), F32),
-            jax.ShapeDtypeStruct(parts_shape, BF16),
+            pltpu.VMEM((local_users, hidden), F32),
+            pltpu.VMEM(parts_shape, BF16),
         ],
         compiler_params=params(8 * MIB),
         name="positive_rows",
     )(exchange(positive_part), bias_row)
     pos_a = exchange(sent)
-    pos_b = lax.ppermute(pos_a, "user", swap)
-
-    negative_part, stats_a = pl.pallas_call(
+
+    negative_part, stats_a, positive_out = pl.pallas_call(
         negative_kernel,
-        in_specs=[vmem, table_spec, vmem, vmem],
-        out_specs=[vmem, vmem],
+        in_specs=[vmem, table_spec, vmem, vmem, vmem, vmem],
+        out_specs=[vmem, vmem, pl.BlockSpec(memory_space=pltpu.HBM)],
         out_shape=[
-            jax.ShapeDtypeStruct(parts_shape, SENT),
+            pltpu.VMEM(parts_shape, BF16),
             jax.ShapeDtypeStruct((columns, LANES), BF16),
+            jax.ShapeDtypeStruct(positive_own.shape, F32),
         ],
         scratch_shapes=[
             table_scratch,
             pltpu.VMEM((hidden, LANES), BF16),
+            pltpu.VMEM((local_movies, 8), F32),
             total_scratch,
-            pltpu.SemaphoreType.DMA((local_movies // tile, levels)),
+            pltpu.SemaphoreType.DMA((len(movie_tiles(tile, local_movies)), levels)),
+            pltpu.SemaphoreType.DMA,
         ],
         compiler_params=params(32 * MIB),
         cost_estimate=pl.CostEstimate(flops=2 * matmul, bytes_accessed=table_bytes, transcendentals=0),
         name="negative",
-    )(pos_a, table, vis_rows, rating)
+    )(pos_a, table, head, vis_bias, rating, positive_own)
     stats_a = stats_a.reshape(levels, local_movies, LANES)
     stats_b = lax.ppermute(stats_a, "user", swap)
 
     sent = pl.pallas_call(
         negative_rows_kernel,
-        in_specs=[vmem, vmem, vmem, pl.BlockSpec(memory_space=pl.ANY)],
-        out_shape=jax.ShapeDtypeStruct((owners, local_users, hidden + 2 * hidden // local_users), BF16),
+        out_shape=pltpu.VMEM((owners, local_users, hidden + 2 * hidden // local_users), BF16),
         compiler_params=params(8 * MIB),
         name="negative_rows",
-    )(exchange(negative_part), bias_row, positive_own, pos_b)
-    neg_a = exchange(sent)
-    neg_b = lax.ppermute(neg_a, "user", swap)
-
+    )(exchange(negative_part), bias_row, positive_own)
+    rows_a = pl.pallas_call(
+        gathered_rows_kernel,
+        out_shape=pltpu.VMEM((LANES + 16, hidden), BF16),
+        compiler_params=params(8 * MIB),
+        name="gathered_rows",
+    )(pos_a, exchange(sent))
+    rows_b = lax.ppermute(rows_a, "user", swap)
     weight_grad, visible_grad, hidden_grad = pl.pallas_call(
         gradient_kernel,
-        in_specs=[vmem] * 6,
-        out_specs=[pl.BlockSpec(memory_space=pltpu.HBM), vmem, vmem],
+        in_specs=[vmem, pl.BlockSpec(memory_space=pl.ANY)] + [vmem] * 2,
+        out_specs=[pl.BlockSpec(memory_space=pltpu.HBM)] * 3,
         out_shape=[
             jax.ShapeDtypeStruct(weights.shape, F32),
             jax.ShapeDtypeStruct((levels, local_movies), F32),
             jax.ShapeDtypeStruct((1, hidden), F32),
         ],
         scratch_shapes=[
+            pltpu.VMEM(stats_a.shape, BF16),
+            pltpu.VMEM((levels, local_movies), F32),
+            pltpu.VMEM((1, hidden), F32),
             pltpu.VMEM((local_movies, 2 * LANES), BF16),
             pltpu.VMEM((2 * LANES, hidden), BF16),
-            pltpu.VMEM((3, rows, hidden), F32),
+            pltpu.VMEM((3, part, hidden), F32),
             pltpu.SemaphoreType.DMA((3,)),
+            pltpu.SemaphoreType.DMA((levels,)),
+            pltpu.SemaphoreType.DMA((2,)),
         ],
         compiler_params=params(32 * MIB),
         cost_estimate=pl.CostEstimate(flops=4 * matmul, bytes_accessed=2 * table_bytes, transcendentals=0),
         name="gradient",
-    )(stats_a, stats_b, pos_a, pos_b, neg_a, neg_b)
-    return weight_grad, visible_grad, hidden_grad[0], positive_own
+    )(stats_a, stats_b, rows_a, rows_b)
+    return weight_grad, visible_grad, hidden_grad[0], positive_out
 
 
 def fits_kernels(mesh, local_users, slots, levels, local_movies, hidden):

time: 91.9 us -> 85.4 us (0.929)
  blocking collectives: 38.1 us -> 60.4 us
  waiting for transfers between devices: 19.1 us -> 1.57 us
  starting transfers between devices: 8 us -> 0.14 us
  Pallas kernels: 24.5 us -> 21.5 us
    all_to_all x3 -> x5, blocking collectives: 38.1 us -> 60.4 us  [exchange(): return lax.all_to_all(x, 'movie', split_axis=0, concat_axis=0, tiled=True)]
    all_to_all x2 -> x0, waiting for transfers between devices: 16.7 us -> none  [exchange(): return lax.all_to_all(x, 'movie', split_axis=0, concat_axis=0, tiled=True)]
    all_to_all x2 -> x0, starting transfers between devices: 7.38 us -> none  [exchange(): return lax.all_to_all(x, 'movie', split_axis=0, concat_axis=0, tiled=True)]
    pallas_call x4 -> x5, Pallas kernels: 19.5 us -> 16.6 us  [the longest x1 8.73 us: on_device_kernels(): pl.pallas_call(gradient_kernel, in_specs=[vmem, pl.BlockSpec(memory_space...]
    ppermute x2 -> x1, waiting for transfers between devices: 2.43 us -> 1.57 us  [on_device_kernels(): rows_b = lax.ppermute(rows_a, 'user', swap)]
  transfers between devices with their start and end apart: 5 -> 2, of which waited for: 4 -> 1; matrix products, arithmetic and copies ran while one was open for 0% -> 0% of each run, Pallas kernels for 0% -> 0%
where the time goes in v2:
time: 85.4 us; the launch traced here: 85 us
  blocking collectives  60.4 us (71%)
  Pallas kernels  21.5 us (25%)
  waiting for transfers between devices  1.57 us (2%)
    all_to_all x5, blocking collectives, exchange(): return lax.all_to_all(x, 'movie', split_axis=0, concat_axis=0, tiled=True)  60.4 us
    pallas_call x1, Pallas kernels, on_device_kernels(): pl.pallas_call(gradient_kernel, in_specs=[vmem, pl.BlockSpec(memory_space...  8.73 us
    pallas_call x1, Pallas kernels, on_device_kernels(): pl.pallas_call(negative_kernel, in_specs=[vmem, table_spec, vmem, vmem, v...  7.63 us
    pallas_call x1, Pallas kernels, on_device_kernels(): pl.pallas_call(positive_kernel, in_specs=[vmem, table_spec], out_specs=[v...  4.95 us
  transfers between devices with their start and end apart: 2, of which 1 were waited for; matrix products, arithmetic and copies ran while one was open for 0% of the time, Pallas kernels for 0%

profile of v2, /device:TPU:0, one launch (start us, length us, event | category | flops | bytes accessed | tf_op | source)
XLA Modules:
  0.0 85.0 jit_solution(5618751201137084867)
XLA Ops:
  0.6 0.7 add_select_fusion
  1.4 15.5 %all_to_all.25.codes_ref = s32[16,4,128]{2,1,0:T(4,128)S(1)} all-to-all(s32[16,4,128]{2,1,0:T(4,128)S(1)} %broadcast_in_dim.14), channel_id=1, replica_groups=mesh['movie'=16,'user'=2] {'movie'}, dimensions={0} | all-to-all | bytes 65536 | tf_op jit(solution)/shard_map/all_to_all | solution.py:250
  16.9 0.0 copy-start.1
  16.9 0.0 copy-start
  16.9 5.0 %positive.1 = (f32[16,4,1024]{2,1,0:T(4,128)S(1)}, bf16[1120,128]{1,0:T(8,128)(2,1)S(1)}, bf16[800,1024]{1,0:T(8,128)(2,1)S(1)}) custom-call(s32[16,4,128]{2,1,0:T(4,128)S(1)} %all_to_all.25.codes_ref, bf16[5600,1024]{1,0:T(8,128)(2,1)} %bitcast.8), custom_call_target="tpu_custom_call" | custom-call | flops 734003200 | bytes 11468800 | tf_op jit(solution)/shard_map/positive/pallas_call | solution.py:289
  21.9 11.1 %all_to_all.26.parts_ref = f32[16,4,1024]{2,1,0:T(4,128)S(1)} all-to-all(f32[16,4,1024]{2,1,0:T(4,128)S(1)} %get-tuple-element.15), channel_id=1, replica_groups=mesh['movie'=16,'user'=2] {'movie'}, dimensions={0} | all-to-all | bytes 524288 | tf_op jit(solution)/shard_map/all_to_all | solution.py:250
  33.0 0.0 copy-done.1
  33.0 11.3 %all_to_all.27.rows_ref.pos_ref = bf16[16,4,1024]{2,1,0:T(4,128)(2,1)S(1)} all-to-all(bf16[16,4,1024]{2,1,0:T(4,128)(2,1)S(1)} %get-tuple-element.16), channel_id=1, replica_groups=mesh['movie'=16,'user'=2] {'movie'}, dimensions={0} | all-to-all | bytes 262144 | tf_op jit(solution)/shard_map/all_to_all | solution.py:250
  44.3 0.0 copy-done
  44.3 7.6 %negative.1 = (bf16[16,4,1024]{2,1,0:T(4,128)(2,1)S(1)}, bf16[5600,128]{1,0:T(8,128)(2,1)S(1)}, f32[4,1024]{1,0:T(4,128)}) custom-call(bf16[16,4,1024]{2,1,0:T(4,128)(2,1)S(1)} %all_to_all.27.rows_ref.pos_ref, bf16[5600,1024]{1,0:T(8,128)(2,1)} %bitcast.9, bf16[800,1024]{1,0:T(8,128)(2,1)S(1)} %get-tuple-element.17.head, f32[5,1120]{1,0:T(8,128)S(1)} %copy-done, ...), custom_call_target="tpu_custom_call" | custom-call | flops 1468006400 | bytes 11468800 | tf_op jit(solution)/shard_map/negative/pallas_call | solution.py:322
  52.0 0.1 collective-permute-start
  52.0 10.9 %all_to_all.28.parts_ref = bf16[16,4,1024]{2,1,0:T(4,128)(2,1)S(1)} all-to-all(bf16[16,4,1024]{2,1,0:T(4,128)(2,1)S(1)} %get-tuple-element.21), channel_id=1, replica_groups=mesh['movie'=16,'user'=2] {'movie'}, dimensions={0} | all-to-all | bytes 262144 | tf_op jit(solution)/shard_map/all_to_all | solution.py:250
  63.0 0.1 negative_rows.1
  63.0 11.5 %all_to_all.29.neg_ref = bf16[16,4,1536]{2,1,0:T(4,128)(2,1)S(1)} all-to-all(bf16[16,4,1536]{2,1,0:T(4,128)(2,1)S(1)} %negative_rows.1), channel_id=1, replica_groups=mesh['movie'=16,'user'=2] {'movie'}, dimensions={0} | all-to-all | bytes 393216 | tf_op jit(solution)/shard_map/all_to_all | solution.py:250
  74.6 0.1 gathered_rows.1.rows_a
  74.7 0.1 collective-permute-start.1
  74.7 1.6 %collective-permute-done.1.rows_b = bf16[144,1024]{1,0:T(8,128)(2,1)S(1)} collective-permute-done((bf16[144,1024]{1,0:T(8,128)(2,1)S(1)}, bf16[144,1024]{1,0:T(8,128)(2,1)S(1)}, u32[]{:S(2)}, u32[]{:S(2)}) %collective-permute-start.1) | collective-permute-done | bytes 294944 | tf_op jit(solution)/shard_map/ppermute | solution.py:358
  76.3 0.0 collective-permute-done.stats_b
  76.3 8.7 %gradient.1 = (f32[5,1120,1024]{2,1,0:T(8,128)}, f32[5,1120]{1,0:T(8,128)}, f32[1,1024]{1,0:T(1,128)}) custom-call(bf16[5,1120,128]{2,1,0:T(8,128)(2,1)S(1)} %bitcast.7, bf16[5,1120,128]{2,1,0:T(8,128)(2,1)S(1)} %collective-permute-done.stats_b, bf16[144,1024]{1,0:T(8,128)(2,1)S(1)} %gathered_rows.1.rows_a, bf16[144,1024]{1,0:T(8,128)(2,1)S(1)} %collective-permute-done.1.rows_b), custom_call_target="tpu_custom_call" | custom-call | flops 2936012800 | bytes 22937600 | tf_op jit(solution)/shard_map/gradient/pallas_call | solution.py:359
  (2 shorter events, 0.0 us)
Async XLA Ops:
  16.9 16.1 %copy-start.1 = (f32[1024]{0:T(1024)S(1)}, f32[1024]{0:T(1024)}, u32[]{:S(2)}) copy-start(f32[1024]{0:T(1024)} %param.11) | copy-start | bytes 12292
  16.9 27.4 %copy-start = (f32[5,1120]{1,0:T(8,128)S(1)}, f32[5,1120]{1,0:T(8,128)}, u32[]{:S(2)}) copy-start(f32[5,1120]{1,0:T(8,128)} %bias_ref.1) | copy-start | bytes 67204
  52.0 24.4 %collective-permute-start = (bf16[5,1120,128]{2,1,0:T(8,128)(2,1)S(1)}, bf16[5,1120,128]{2,1,0:T(8,128)(2,1)S(1)}, u32[]{:S(2)}, u32[]{:S(2)}) collective-permute-start(bf16[5,1120,128]{2,1,0:T(8,128)(2,1)S(1)} %bitcast.6), channel_id=1, source_target_pairs={{0,1},{1,0},{2,3},{3,2},{4,5},{5,4},{6,7},{7,6},{8,9},{9,8},{10,11... | collective-permute-start | bytes 4300808 | tf_op jit(solution)/shard_map/ppermute | solution.py:344
  74.7 1.6 %collective-permute-start.1 = (bf16[144,1024]{1,0:T(8,128)(2,1)S(1)}, bf16[144,1024]{1,0:T(8,128)(2,1)S(1)}, u32[]{:S(2)}, u32[]{:S(2)}) collective-permute-start(bf16[144,1024]{1,0:T(8,128)(2,1)S(1)} %gathered_rows.1.rows_a), channel_id=1, source_target_pairs={{0,1},{1,0},{2,3},{3,2},{4,5},{5,4},{6,7},{7,6},{8,9},{9,8},{10,11... | collective-permute-start | bytes 884744 | tf_op jit(solution)/shard_map/ppermute | solution.py:358

commit v3 on v2

--- a/solution.py
+++ b/solution.py
@@ -114,7 +114,7 @@
 
     ready = logits(0)
     for t, (start, tile) in enumerate(tiles):
-        following = logits(t + 1) if t + 1 < len(tiles) else None
+        following = logits(t + 1) if t < len(tiles) - 1 else None
         first = lax.broadcasted_iota(jnp.int32, (tile, LANES), 1) < LANES // 2
         own = slice(start, start + tile)
         bias = bias_s[own, :]
@@ -154,14 +154,13 @@
 
 def negative_rows_kernel(parts_ref, bias_ref, positive_ref, sent_ref):
     sources, local_users, hidden = parts_ref.shape
-    side = 2 * hidden // local_users
+    side = hidden // local_users
     summed = functools.reduce(jnp.add, [parts_ref[i].astype(F32) for i in range(sources)])
     own = jax.nn.sigmoid(bias_ref[...] + summed)
-    difference = jnp.sum(positive_ref[...] - own, axis=0, keepdims=True)
-    high = difference.astype(BF16).astype(F32)
-    rest = difference - high
-    pieces = hidden // side
-    split = [x[:, i * side : (i + 1) * side] for x in (high, rest) for i in range(pieces)]
+    positive = positive_ref[...]
+    lost = (positive - positive.astype(BF16).astype(F32)) - (own - own.astype(BF16).astype(F32))
+    lost = jnp.sum(lost, axis=0, keepdims=True)
+    split = [lost[:, i * side : (i + 1) * side] for i in range(local_users)]
     low = jnp.concatenate([own, jnp.concatenate(split, axis=0)], axis=1).astype(BF16)
     for i in range(sources):
         sent_ref[i] = low
@@ -172,9 +171,7 @@
     wide = [neg_ref[i].astype(F32) for i in range(sources)]
     block = [pos_ref[i].astype(F32) for i in range(sources)] + [x[:, :hidden] for x in wide]
     sides = functools.reduce(jnp.add, [x[:, hidden:] for x in wide])
-    pieces = sides.shape[0] // 2
-    sides = sides[:pieces] + sides[pieces:]
-    rest = jnp.concatenate([sides[i : i + 1] for i in range(pieces)], axis=1)
+    rest = jnp.concatenate([sides[i : i + 1] for i in range(sides.shape[0])], axis=1)
     terms = []
     for _ in range(3):
         terms.append(rest.astype(BF16).astype(F32))
@@ -183,31 +180,45 @@
     rows_ref[...] = jnp.concatenate(block + terms + [spare], axis=0).astype(BF16)
 
 
-def gradient_kernel(stats_a, stats_b, rows_a, rows_b, target, visible_out, hidden_out, stats_s, visible_ref, hidden_ref, lhs, rhs, slots, sent, got, done):
+def halves():
+    mine = pl.multiple_of(lax.axis_index("user") * LANES, LANES)
+    return mine, pl.multiple_of(LANES - mine, LANES)
+
+
+def first_level_kernel(stats_a, stats_b, lhs_ref, other_s, arrived):
+    mine, other = halves()
+    copy = pltpu.make_async_copy(stats_b.at[0], other_s, arrived)
+    copy.start()
+    lhs_ref[:, pl.ds(mine, LANES)] = stats_a[0]
+    copy.wait()
+    lhs_ref[:, pl.ds(other, LANES)] = other_s[...]
+
+
+def gradient_kernel(stats_a, stats_b, first, rows_a, rows_b, target, visible_out, hidden_out, stats_s, visible_ref, hidden_ref, lhs, rhs, slots, sent, got, done):
     levels, local_movies, _ = stats_a.shape
     buffers, rows, _ = slots.shape
     parts = local_movies // rows
-    mine = pl.multiple_of(lax.axis_index("user") * LANES, LANES)
-    other = pl.multiple_of(LANES - mine, LANES)
-
-    fetch = [pltpu.make_async_copy(stats_b.at[i], stats_s.at[i], got.at[i]) for i in range(levels)]
+    mine, other = halves()
+
+    fetch = [pltpu.make_async_copy(stats_b.at[i], stats_s.at[i], got.at[i]) for i in range(1, levels)]
     for copy in fetch:
         copy.start()
     rhs[pl.ds(mine, LANES), :] = rows_a[:LANES, :]
     rhs[pl.ds(other, LANES), :] = rows_b[:LANES, :]
-    sums = [jnp.sum(ref[LANES:, :].astype(F32), axis=0, keepdims=True) for ref in (rows_a, rows_b)]
-    hidden_ref[...] = sums[0] + sums[1]
-    ones = jnp.ones((8, LANES), BF16)
+    lhs[...] = first[...]
+    ones = jnp.ones((8, 2 * LANES), BF16)
 
     def send(level, part, slot):
         place = target.at[level, pl.ds(part * rows, rows)]
         return pltpu.make_async_copy(slots.at[slot], place, sent.at[slot])
 
     def one_level(level, carry):
-        pltpu.make_async_copy(stats_b.at[level], stats_s.at[level], got.at[level]).wait()
-        a, b = stats_a[level], stats_s[level]
-        lhs[:, pl.ds(mine, LANES)] = a
-        lhs[:, pl.ds(other, LANES)] = b
+        @pl.when(level > 0)
+        def _():
+            pltpu.make_async_copy(stats_b.at[level], stats_s.at[level], got.at[level]).wait()
+            lhs[:, pl.ds(mine, LANES)] = stats_a[level]
+            lhs[:, pl.ds(other, LANES)] = stats_s[level]
+
         for part in range(parts):
             count = level * parts + part
             slot = lax.rem(count, buffers)
@@ -219,13 +230,20 @@
             block = lhs[part * rows : (part + 1) * rows, :]
             slots[slot] = jnp.dot(block, rhs[...], preferred_element_type=F32)
             send(level, part, slot).start()
-        summed = lax.dot_general(ones, a, NT, preferred_element_type=F32) + lax.dot_general(
-            ones, b, NT, preferred_element_type=F32
-        )
+        summed = lax.dot_general(ones, lhs[...], NT, preferred_element_type=F32)
         visible_ref[pl.ds(level, 1), :] = summed[:1]
         return carry
 
     lax.fori_loop(0, levels, one_level, 0)
+
+    def total(ref, first, last):
+        return jnp.sum(ref[first:last, :].astype(F32), axis=0, keepdims=True)
+
+    users = LANES // 2
+    sums = [
+        total(ref, 0, users) - total(ref, users, LANES) + total(ref, LANES, LANES + 16) for ref in (rows_a, rows_b)
+    ]
+    hidden_ref[...] = sums[0] + sums[1]
     small = [
         pltpu.make_async_copy(visible_ref, visible_out, done.at[0]),
         pltpu.make_async_copy(hidden_ref, hidden_out, done.at[1]),
@@ -259,8 +277,9 @@
 
 def movie_tiles(held, movies):
     wide, left = divmod(movies - held, WIDE_TILE)
-    sizes = [held] + [WIDE_TILE] * wide
-    sizes += [left // 2] * 2 if left and left % 32 == 0 else [left] * (left > 0)
+    edge = left // 2 if left % 32 == 0 else left
+    sizes = [held, edge] + [WIDE_TILE] * wide + [left - edge]
+    sizes = [size for size in sizes if size]
     return [(sum(sizes[:i]), size) for i, size in enumerate(sizes)]
 
 
@@ -345,7 +364,7 @@
 
     sent = pl.pallas_call(
         negative_rows_kernel,
-        out_shape=pltpu.VMEM((owners, local_users, hidden + 2 * hidden // local_users), BF16),
+        out_shape=pltpu.VMEM((owners, local_users, hidden + hidden // local_users), BF16),
         compiler_params=params(8 * MIB),
         name="negative_rows",
     )(exchange(negative_part), bias_row, positive_own)
@@ -356,9 +375,19 @@
         name="gathered_rows",
     )(pos_a, exchange(sent))
     rows_b = lax.ppermute(rows_a, "user", swap)
+    first = pl.pallas_call(
+        first_level_kernel,
+        in_specs=[vmem, pl.BlockSpec(memory_space=pl.ANY)],
+        out_specs=vmem,
+        out_shape=pltpu.VMEM((local_movies, 2 * LANES), BF16),
+        scratch_shapes=[pltpu.VMEM((local_movies, LANES), BF16), pltpu.SemaphoreType.DMA],
+        compiler_params=params(8 * MIB),
+        cost_estimate=pl.CostEstimate(flops=1 << 27, bytes_accessed=1 << 20, transcendentals=0),
+        name="first_level",
+    )(stats_a, stats_b)
     weight_grad, visible_grad, hidden_grad = pl.pallas_call(
         gradient_kernel,
-        in_specs=[vmem, pl.BlockSpec(memory_space=pl.ANY)] + [vmem] * 2,
+        in_specs=[vmem, pl.BlockSpec(memory_space=pl.ANY)] + [vmem] * 3,
         out_specs=[pl.BlockSpec(memory_space=pltpu.HBM)] * 3,
         out_shape=[
             jax.ShapeDtypeStruct(weights.shape, F32),
@@ -379,7 +408,7 @@
         compiler_params=params(32 * MIB),
         cost_estimate=pl.CostEstimate(flops=4 * matmul, bytes_accessed=2 * table_bytes, transcendentals=0),
         name="gradient",
-    )(stats_a, stats_b, rows_a, rows_b)
+    )(stats_a, stats_b, first, rows_a, rows_b)
     return weight_grad, visible_grad, hidden_grad[0], positive_out
 
 

time: 85.4 us -> 84.2 us (0.986)
  no operation moved by 1% of the time
where the time goes in v3:
time: 84.2 us; the launch traced here: 83.9 us
  blocking collectives  59.7 us (71%)
  Pallas kernels  21.2 us (25%)
  waiting for transfers between devices  1.39 us (2%)
    all_to_all x5, blocking collectives, exchange(): return lax.all_to_all(x, 'movie', split_axis=0, concat_axis=0, tiled=True)  59.7 us
    pallas_call x1, Pallas kernels, on_device_kernels(): pl.pallas_call(gradient_kernel, in_specs=[vmem, pl.BlockSpec(memory_space...  8.56 us
    pallas_call x1, Pallas kernels, on_device_kernels(): pl.pallas_call(negative_kernel, in_specs=[vmem, table_spec, vmem, vmem, v...  7.36 us
    pallas_call x1, Pallas kernels, on_device_kernels(): pl.pallas_call(positive_kernel, in_specs=[vmem, table_spec], out_specs=[v...  4.95 us
  transfers between devices with their start and end apart: 2, of which 1 were waited for; matrix products, arithmetic and copies ran while one was open for 0% of the time, Pallas kernels for 0%

profile of v3, /device:TPU:0, one launch (start us, length us, event | category | flops | bytes accessed | tf_op | source)
XLA Modules:
  0.0 83.9 jit_solution(4050561669110065917)
XLA Ops:
  0.6 0.7 add_select_fusion
  1.4 15.5 %all_to_all.25.codes_ref = s32[16,4,128]{2,1,0:T(4,128)S(1)} all-to-all(s32[16,4,128]{2,1,0:T(4,128)S(1)} %broadcast_in_dim.14), channel_id=1, replica_groups=mesh['movie'=16,'user'=2] {'movie'}, dimensions={0} | all-to-all | bytes 65536 | tf_op jit(solution)/shard_map/all_to_all | solution.py:268
  16.9 0.0 copy-start.1
  16.9 0.0 copy-start
  16.9 5.0 %positive.1 = (f32[16,4,1024]{2,1,0:T(4,128)S(1)}, bf16[1120,128]{1,0:T(8,128)(2,1)S(1)}, bf16[800,1024]{1,0:T(8,128)(2,1)S(1)}) custom-call(s32[16,4,128]{2,1,0:T(4,128)S(1)} %all_to_all.25.codes_ref, bf16[5600,1024]{1,0:T(8,128)(2,1)} %bitcast.9), custom_call_target="tpu_custom_call" | custom-call | flops 734003200 | bytes 11468800 | tf_op jit(solution)/shard_map/positive/pallas_call | solution.py:308
  21.9 11.1 %all_to_all.26.parts_ref = f32[16,4,1024]{2,1,0:T(4,128)S(1)} all-to-all(f32[16,4,1024]{2,1,0:T(4,128)S(1)} %get-tuple-element.15), channel_id=1, replica_groups=mesh['movie'=16,'user'=2] {'movie'}, dimensions={0} | all-to-all | bytes 524288 | tf_op jit(solution)/shard_map/all_to_all | solution.py:268
  33.0 0.0 copy-done.1
  33.0 11.3 %all_to_all.27.rows_ref.pos_ref = bf16[16,4,1024]{2,1,0:T(4,128)(2,1)S(1)} all-to-all(bf16[16,4,1024]{2,1,0:T(4,128)(2,1)S(1)} %get-tuple-element.16), channel_id=1, replica_groups=mesh['movie'=16,'user'=2] {'movie'}, dimensions={0} | all-to-all | bytes 262144 | tf_op jit(solution)/shard_map/all_to_all | solution.py:268
  44.3 0.0 copy-done
  44.3 7.4 %negative.1 = (bf16[16,4,1024]{2,1,0:T(4,128)(2,1)S(1)}, bf16[5600,128]{1,0:T(8,128)(2,1)S(1)}, f32[4,1024]{1,0:T(4,128)}) custom-call(bf16[16,4,1024]{2,1,0:T(4,128)(2,1)S(1)} %all_to_all.27.rows_ref.pos_ref, bf16[5600,1024]{1,0:T(8,128)(2,1)} %bitcast.10, bf16[800,1024]{1,0:T(8,128)(2,1)S(1)} %get-tuple-element.17.head, f32[5,1120]{1,0:T(8,128)S(1)} %copy-done, ...), custom_call_target="tpu_custom_call" | custom-call | flops 1468006400 | bytes 11468800 | tf_op jit(solution)/shard_map/negative/pallas_call | solution.py:341
  51.7 0.1 collective-permute-start
  51.8 10.9 %all_to_all.28.parts_ref = bf16[16,4,1024]{2,1,0:T(4,128)(2,1)S(1)} all-to-all(bf16[16,4,1024]{2,1,0:T(4,128)(2,1)S(1)} %get-tuple-element.21), channel_id=1, replica_groups=mesh['movie'=16,'user'=2] {'movie'}, dimensions={0} | all-to-all | bytes 262144 | tf_op jit(solution)/shard_map/all_to_all | solution.py:268
  62.7 0.1 negative_rows.1
  62.8 10.9 %all_to_all.29.neg_ref = bf16[16,4,1280]{2,1,0:T(4,128)(2,1)S(1)} all-to-all(bf16[16,4,1280]{2,1,0:T(4,128)(2,1)S(1)} %negative_rows.1), channel_id=1, replica_groups=mesh['movie'=16,'user'=2] {'movie'}, dimensions={0} | all-to-all | bytes 327680 | tf_op jit(solution)/shard_map/all_to_all | solution.py:268
  73.6 0.1 gathered_rows.1.rows_a
  73.7 0.1 collective-permute-start.1
  73.8 0.0 collective-permute-done.stats_b
  73.8 0.2 first_level.1.first
  74.0 1.4 %collective-permute-done.1.rows_b = bf16[144,1024]{1,0:T(8,128)(2,1)S(1)} collective-permute-done((bf16[144,1024]{1,0:T(8,128)(2,1)S(1)}, bf16[144,1024]{1,0:T(8,128)(2,1)S(1)}, u32[]{:S(2)}, u32[]{:S(2)}) %collective-permute-start.1) | collective-permute-done | bytes 294944 | tf_op jit(solution)/shard_map/ppermute | solution.py:377
  75.4 8.6 %gradient.1 = (f32[5,1120,1024]{2,1,0:T(8,128)}, f32[5,1120]{1,0:T(8,128)}, f32[1,1024]{1,0:T(1,128)}) custom-call(bf16[5,1120,128]{2,1,0:T(8,128)(2,1)S(1)} %bitcast.6, bf16[5,1120,128]{2,1,0:T(8,128)(2,1)S(1)} %collective-permute-done.stats_b, bf16[1120,256]{1,0:T(8,128)(2,1)S(1)} %first_level.1.first, bf16[144,1024]{1,0:T(8,128)(2,1)S(1)} %gathered_rows.1.rows_a, ...), custom_call_target="tpu_custom_call" | custom-call | flops 2936012800 | bytes 22937600 | tf_op jit(solution)/shard_map/gradient/pallas_call | solution.py:388
  (2 shorter events, 0.0 us)
Async XLA Ops:
  16.9 16.1 %copy-start.1 = (f32[1024]{0:T(1024)S(1)}, f32[1024]{0:T(1024)}, u32[]{:S(2)}) copy-start(f32[1024]{0:T(1024)} %param.11) | copy-start | bytes 12292
  16.9 27.4 %copy-start = (f32[5,1120]{1,0:T(8,128)S(1)}, f32[5,1120]{1,0:T(8,128)}, u32[]{:S(2)}) copy-start(f32[5,1120]{1,0:T(8,128)} %bias_ref.1) | copy-start | bytes 67204
  51.7 22.1 %collective-permute-start = (bf16[5,1120,128]{2,1,0:T(8,128)(2,1)S(1)}, bf16[5,1120,128]{2,1,0:T(8,128)(2,1)S(1)}, u32[]{:S(2)}, u32[]{:S(2)}) collective-permute-start(bf16[5,1120,128]{2,1,0:T(8,128)(2,1)S(1)} %bitcast.4), channel_id=1, source_target_pairs={{0,1},{1,0},{2,3},{3,2},{4,5},{5,4},{6,7},{7,6},{8,9},{9,8},{10,11... | collective-permute-start | bytes 4300808 | tf_op jit(solution)/shard_map/ppermute | solution.py:363
  73.7 1.6 %collective-permute-start.1 = (bf16[144,1024]{1,0:T(8,128)(2,1)S(1)}, bf16[144,1024]{1,0:T(8,128)(2,1)S(1)}, u32[]{:S(2)}, u32[]{:S(2)}) collective-permute-start(bf16[144,1024]{1,0:T(8,128)(2,1)S(1)} %gathered_rows.1.rows_a), channel_id=1, source_target_pairs={{0,1},{1,0},{2,3},{3,2},{4,5},{5,4},{6,7},{7,6},{8,9},{9,8},{10,11... | collective-permute-start | bytes 884744 | tf_op jit(solution)/shard_map/ppermute | solution.py:377

commit v4 on v3

--- a/solution.py
+++ b/solution.py
@@ -26,14 +26,17 @@
     tile = head.shape[0] // levels
     rest = local_movies - tile
     blocks = [(0, levels * tile, head, 0)]
-    blocks += [(levels * tile + k * rest, rest, table, k * rest) for k in range(levels)]
+    last = min(WIDE_TILE, rest // 2)
+    runs = [(k * rest, rest) for k in range(levels - 1)]
+    runs += [((levels - 1) * rest, rest - last), (levels * rest - last, last)]
+    blocks += [(levels * tile + at, size, table, at) for at, size in runs]
     copies = []
     for k in range(levels):
         first = k * local_movies
         copies.append((source.at[pl.ds(first, tile)], head.at[pl.ds(k * tile, tile)]))
-    for k in range(levels):
-        first = k * local_movies + tile
-        copies.append((source.at[pl.ds(first, rest)], table.at[pl.ds(k * rest, rest)]))
+    for at, size in runs:
+        first = at + tile * (at // rest + 1)
+        copies.append((source.at[pl.ds(first, size)], table.at[pl.ds(at, size)]))
     copies = [pltpu.make_async_copy(*pair, arrived.at[i]) for i, pair in enumerate(copies)]
     for copy in copies:
         copy.start()
@@ -213,28 +216,37 @@
         return pltpu.make_async_copy(slots.at[slot], place, sent.at[slot])
 
     def one_level(level, carry):
-        @pl.when(level > 0)
-        def _():
+        if not isinstance(level, int):
             pltpu.make_async_copy(stats_b.at[level], stats_s.at[level], got.at[level]).wait()
             lhs[:, pl.ds(mine, LANES)] = stats_a[level]
             lhs[:, pl.ds(other, LANES)] = stats_s[level]
 
         for part in range(parts):
             count = level * parts + part
-            slot = lax.rem(count, buffers)
-
-            @pl.when(count >= buffers)
-            def _():
-                send(level, part, slot).wait()
-
-            block = lhs[part * rows : (part + 1) * rows, :]
-            slots[slot] = jnp.dot(block, rhs[...], preferred_element_type=F32)
-            send(level, part, slot).start()
+            slot = count % buffers if isinstance(count, int) else lax.rem(count, buffers)
+            if isinstance(count, int):
+                if count >= buffers:
+                    send(level, part, slot).wait()
+            else:
+
+                @pl.when(count >= buffers)
+                def _():
+                    send(level, part, slot).wait()
+
+            edges = [0, rows]
+            if isinstance(level, int) and part == 0 and rows > 2 * LANES:
+                edges = [0, LANES, rows]
+            for low, high in zip(edges, edges[1:]):
+                block = lhs[part * rows + low : part * rows + high, :]
+                slots[slot, low:high] = jnp.dot(block, rhs[...], preferred_element_type=F32)
+                place = target.at[level, pl.ds(part * rows + low, high - low)]
+                pltpu.make_async_copy(slots.at[slot, pl.ds(low, high - low)], place, sent.at[slot]).start()
         summed = lax.dot_general(ones, lhs[...], NT, preferred_element_type=F32)
         visible_ref[pl.ds(level, 1), :] = summed[:1]
         return carry
 
-    lax.fori_loop(0, levels, one_level, 0)
+    one_level(0, 0)
+    lax.fori_loop(1, levels, one_level, 0)
 
     def total(ref, first, last):
         return jnp.sum(ref[first:last, :].astype(F32), axis=0, keepdims=True)
@@ -320,7 +332,7 @@
             pltpu.VMEM((slots // 2, LANES), F32),
             pltpu.VMEM((slots // 2, LANES), F32),
             total_scratch,
-            pltpu.SemaphoreType.DMA((2 * levels,)),
+            pltpu.SemaphoreType.DMA((2 * levels + 1,)),
         ],
         compiler_params=params(32 * MIB),
         cost_estimate=pl.CostEstimate(flops=matmul, bytes_accessed=table_bytes, transcendentals=0),

time: 84.2 us -> 84.1 us (level)
  no operation moved by 1% of the time
where the time goes in v4:
time: 84.1 us; the launch traced here: 83.7 us
  blocking collectives  59.8 us (71%)
  Pallas kernels  21 us (25%)
  waiting for transfers between devices  1.39 us (2%)
    all_to_all x5, blocking collectives, exchange(): return lax.all_to_all(x, 'movie', split_axis=0, concat_axis=0, tiled=True)  59.8 us
    pallas_call x1, Pallas kernels, on_device_kernels(): pl.pallas_call(gradient_kernel, in_specs=[vmem, pl.BlockSpec(memory_space...  8.39 us
    pallas_call x1, Pallas kernels, on_device_kernels(): pl.pallas_call(negative_kernel, in_specs=[vmem, table_spec, vmem, vmem, v...  7.36 us
    pallas_call x1, Pallas kernels, on_device_kernels(): pl.pallas_call(positive_kernel, in_specs=[vmem, table_spec], out_specs=[v...  4.93 us
  transfers between devices with their start and end apart: 2, of which 1 were waited for; matrix products, arithmetic and copies ran while one was open for 0% of the time, Pallas kernels for 0%

profile of v4, /device:TPU:0, one launch (start us, length us, event | category | flops | bytes accessed | tf_op | source)
XLA Modules:
  0.0 83.7 jit_solution(17182649718270833328)
XLA Ops:
  0.6 0.7 add_select_fusion
  1.4 15.5 %all_to_all.25.codes_ref = s32[16,4,128]{2,1,0:T(4,128)S(1)} all-to-all(s32[16,4,128]{2,1,0:T(4,128)S(1)} %broadcast_in_dim.14), channel_id=1, replica_groups=mesh['movie'=16,'user'=2] {'movie'}, dimensions={0} | all-to-all | bytes 65536 | tf_op jit(solution)/shard_map/all_to_all | solution.py:280
  16.9 0.0 copy-start.1
  16.9 0.0 copy-start
  16.9 4.9 %positive.1 = (f32[16,4,1024]{2,1,0:T(4,128)S(1)}, bf16[1120,128]{1,0:T(8,128)(2,1)S(1)}, bf16[800,1024]{1,0:T(8,128)(2,1)S(1)}) custom-call(s32[16,4,128]{2,1,0:T(4,128)S(1)} %all_to_all.25.codes_ref, bf16[5600,1024]{1,0:T(8,128)(2,1)} %bitcast.9), custom_call_target="tpu_custom_call" | custom-call | flops 734003200 | bytes 11468800 | tf_op jit(solution)/shard_map/positive/pallas_call | solution.py:320
  21.8 11.1 %all_to_all.26.parts_ref = f32[16,4,1024]{2,1,0:T(4,128)S(1)} all-to-all(f32[16,4,1024]{2,1,0:T(4,128)S(1)} %get-tuple-element.15), channel_id=1, replica_groups=mesh['movie'=16,'user'=2] {'movie'}, dimensions={0} | all-to-all | bytes 524288 | tf_op jit(solution)/shard_map/all_to_all | solution.py:280
  32.9 0.0 copy-done.1
  33.0 11.3 %all_to_all.27.rows_ref.pos_ref = bf16[16,4,1024]{2,1,0:T(4,128)(2,1)S(1)} all-to-all(bf16[16,4,1024]{2,1,0:T(4,128)(2,1)S(1)} %get-tuple-element.16), channel_id=1, replica_groups=mesh['movie'=16,'user'=2] {'movie'}, dimensions={0} | all-to-all | bytes 262144 | tf_op jit(solution)/shard_map/all_to_all | solution.py:280
  44.3 0.0 copy-done
  44.3 7.4 %negative.1 = (bf16[16,4,1024]{2,1,0:T(4,128)(2,1)S(1)}, bf16[5600,128]{1,0:T(8,128)(2,1)S(1)}, f32[4,1024]{1,0:T(4,128)}) custom-call(bf16[16,4,1024]{2,1,0:T(4,128)(2,1)S(1)} %all_to_all.27.rows_ref.pos_ref, bf16[5600,1024]{1,0:T(8,128)(2,1)} %bitcast.10, bf16[800,1024]{1,0:T(8,128)(2,1)S(1)} %get-tuple-element.17.head, f32[5,1120]{1,0:T(8,128)S(1)} %copy-done, ...), custom_call_target="tpu_custom_call" | custom-call | flops 1468006400 | bytes 11468800 | tf_op jit(solution)/shard_map/negative/pallas_call | solution.py:353
  51.7 0.1 collective-permute-start
  51.8 10.9 %all_to_all.28.parts_ref = bf16[16,4,1024]{2,1,0:T(4,128)(2,1)S(1)} all-to-all(bf16[16,4,1024]{2,1,0:T(4,128)(2,1)S(1)} %get-tuple-element.21), channel_id=1, replica_groups=mesh['movie'=16,'user'=2] {'movie'}, dimensions={0} | all-to-all | bytes 262144 | tf_op jit(solution)/shard_map/all_to_all | solution.py:280
  62.7 0.1 negative_rows.1
  62.7 10.9 %all_to_all.29.neg_ref = bf16[16,4,1280]{2,1,0:T(4,128)(2,1)S(1)} all-to-all(bf16[16,4,1280]{2,1,0:T(4,128)(2,1)S(1)} %negative_rows.1), channel_id=1, replica_groups=mesh['movie'=16,'user'=2] {'movie'}, dimensions={0} | all-to-all | bytes 327680 | tf_op jit(solution)/shard_map/all_to_all | solution.py:280
  73.6 0.1 gathered_rows.1.rows_a
  73.7 0.1 collective-permute-start.1
  73.8 0.0 collective-permute-done.stats_b
  73.8 0.2 first_level.1.first
  74.0 1.4 %collective-permute-done.1.rows_b = bf16[144,1024]{1,0:T(8,128)(2,1)S(1)} collective-permute-done((bf16[144,1024]{1,0:T(8,128)(2,1)S(1)}, bf16[144,1024]{1,0:T(8,128)(2,1)S(1)}, u32[]{:S(2)}, u32[]{:S(2)}) %collective-permute-start.1) | collective-permute-done | bytes 294944 | tf_op jit(solution)/shard_map/ppermute | solution.py:389
  75.4 8.4 %gradient.1 = (f32[5,1120,1024]{2,1,0:T(8,128)}, f32[5,1120]{1,0:T(8,128)}, f32[1,1024]{1,0:T(1,128)}) custom-call(bf16[5,1120,128]{2,1,0:T(8,128)(2,1)S(1)} %bitcast.6, bf16[5,1120,128]{2,1,0:T(8,128)(2,1)S(1)} %collective-permute-done.stats_b, bf16[1120,256]{1,0:T(8,128)(2,1)S(1)} %first_level.1.first, bf16[144,1024]{1,0:T(8,128)(2,1)S(1)} %gathered_rows.1.rows_a, ...), custom_call_target="tpu_custom_call" | custom-call | flops 2936012800 | bytes 22937600 | tf_op jit(solution)/shard_map/gradient/pallas_call | solution.py:400
  (2 shorter events, 0.0 us)
Async XLA Ops:
  16.9 16.0 %copy-start.1 = (f32[1024]{0:T(1024)S(1)}, f32[1024]{0:T(1024)}, u32[]{:S(2)}) copy-start(f32[1024]{0:T(1024)} %param.11) | copy-start | bytes 12292
  16.9 27.4 %copy-start = (f32[5,1120]{1,0:T(8,128)S(1)}, f32[5,1120]{1,0:T(8,128)}, u32[]{:S(2)}) copy-start(f32[5,1120]{1,0:T(8,128)} %bias_ref.1) | copy-start | bytes 67204
  51.7 22.1 %collective-permute-start = (bf16[5,1120,128]{2,1,0:T(8,128)(2,1)S(1)}, bf16[5,1120,128]{2,1,0:T(8,128)(2,1)S(1)}, u32[]{:S(2)}, u32[]{:S(2)}) collective-permute-start(bf16[5,1120,128]{2,1,0:T(8,128)(2,1)S(1)} %bitcast.4), channel_id=1, source_target_pairs={{0,1},{1,0},{2,3},{3,2},{4,5},{5,4},{6,7},{7,6},{8,9},{9,8},{10,11... | collective-permute-start | bytes 4300808 | tf_op jit(solution)/shard_map/ppermute | solution.py:375
  73.7 1.6 %collective-permute-start.1 = (bf16[144,1024]{1,0:T(8,128)(2,1)S(1)}, bf16[144,1024]{1,0:T(8,128)(2,1)S(1)}, u32[]{:S(2)}, u32[]{:S(2)}) collective-permute-start(bf16[144,1024]{1,0:T(8,128)(2,1)S(1)} %gathered_rows.1.rows_a), channel_id=1, source_target_pairs={{0,1},{1,0},{2,3},{3,2},{4,5},{5,4},{6,7},{7,6},{8,9},{9,8},{10,11... | collective-permute-start | bytes 884744 | tf_op jit(solution)/shard_map/ppermute | solution.py:389
